TPU v7x, 512 devices: a whole 4x8x8 slice. The times are simulated.
512 devices in a mesh: outer: 32 (over z_lo, y), inner: 16 (over z_hi, x, core).
Axes of the slice: x: 4, y: 8, z: 8 (z_hi: 2, z_lo: 4; z = z_hi * 4 + z_lo), core: 2. Of those that a mesh axis runs over, the one named last changes fastest.
Arguments:
- tokens: bfloat16 [4096, 4096], P('inner'), may hold values from -6 to 6
- weight_codes: int32 [2, 4096, 14336], P(None, 'inner', 'outer'), may hold values from -127 to 127
- weight_scales: float32 [2, 32, 14336], P(None, 'inner', 'outer'), may hold values from 0.000109375 to 0.0004375
- grad_codes: int32 [2, 4096, 14336], P(None, 'inner', 'outer'), may hold values from -8 to 7
- grad_scales: float32 [2, 32, 14336], P(None, 'inner', 'outer'), may hold values from 0.32 to 57.6
- cotangent: bfloat16 [4096, 14336], P('inner', 'outer'), may hold values from -6 to 6
Outputs:
- hidden: bfloat16 [4096, 14336], P('inner', 'outer')
- input_grad: bfloat16 [4096, 4096], P('inner', 'outer')
- update: float32 [2, 4096, 14336], P(None, 'inner', 'outer')
All inputs are finite; a program needn't handle non-finite values.
Results may differ from a plain program's by a relative error of at most 0.023.
Values may be sent and summed in bfloat16 or wider, within the bound.
A program may use at most 128 MiB of HBM per device.

v0:
```python
import jax
import jax.numpy as jnp
from jax import lax
from jax.sharding import Mesh
from jax.sharding import PartitionSpec as P

D = 4096
FF = 14336
QBLOCK = 128
INNER = ("inner_0", "inner_1", "inner_2")
OUTER = ("outer_0", "outer_1")
OUTER_INNER = ("outer_0", "outer_1", "inner_0", "inner_1", "inner_2")


def reduced_to_own(blocks, axes, order):
    inside = blocks.shape[1:]
    blocks = blocks.reshape(*(lax.axis_size(a) for a in axes), *inside)
    blocks = jnp.moveaxis(blocks, order, range(len(axes))).reshape(-1, *inside)
    for k in order:
        blocks = lax.psum_scatter(blocks, axes[k], scatter_dimension=0, tiled=True)
    return blocks[0]


def split_up(value, dim, length):
    before, after = (value.shape[:dim], value.shape[dim + 1 :])
    return jnp.moveaxis(value.reshape(*before, length, -1, *after), dim, 0)


def scatter_axes(value, axes, order, dim):
    length = lax.axis_size(axes)
    return reduced_to_own(split_up(value, dim, length), axes, order)


def by_axis(value, axes):
    for axis in axes:
        value = lax.psum(value, axis)
    return value


def dequantize(codes, scales):
    count, rows, cols = codes.shape
    blocks = (
        codes.reshape(count, rows // QBLOCK, QBLOCK, cols).astype(jnp.float32)
        * scales[:, :, None, :]
    )
    return blocks.reshape(count, rows, cols)


def local(tokens, weight_codes, weight_scales, grad_codes, grad_scales, cotangent):
    local_rows = dequantize(weight_codes, weight_scales).astype(jnp.bfloat16)
    groups = lax.axis_size(INNER)
    cols = local_rows.shape[2]
    whole = lax.all_gather(local_rows, INNER, axis=1, tiled=True)
    gate = jnp.dot(tokens, whole[0], preferred_element_type=jnp.float32)
    up = jnp.dot(tokens, whole[1], preferred_element_type=jnp.float32)
    sig = jax.nn.sigmoid(gate)
    hidden = (gate * sig * up).astype(jnp.bfloat16)
    back = cotangent.astype(jnp.float32)
    d_gate = (back * up * sig * (1.0 + gate * (1.0 - sig))).astype(jnp.bfloat16)
    d_up = (back * gate * sig).astype(jnp.bfloat16)
    input_term = jnp.dot(d_gate, whole[0].T, preferred_element_type=jnp.float32)
    input_term = input_term + jnp.dot(d_up, whole[1].T, preferred_element_type=jnp.float32)
    input_grad = (
        scatter_axes(input_term.astype(jnp.bfloat16), OUTER, (1, 0), 1)
        .astype(jnp.float32)
        .astype(jnp.bfloat16)
    )
    part_gate = jnp.dot(tokens.T, d_gate, preferred_element_type=jnp.float32).astype(jnp.bfloat16)
    sent_gate = lax.all_to_all(
        part_gate.reshape((groups, part_gate.shape[0] // groups, cols)),
        INNER,
        split_axis=0,
        concat_axis=0,
        tiled=True,
    )
    part_up = jnp.dot(tokens.T, d_up, preferred_element_type=jnp.float32).astype(jnp.bfloat16)
    sent_up = lax.all_to_all(
        part_up.reshape((groups, part_up.shape[0] // groups, cols)),
        INNER,
        split_axis=0,
        concat_axis=0,
        tiled=True,
    )
    grads = jnp.stack(
        [
            jnp.sum(sent_gate.astype(jnp.float32), axis=0),
            jnp.sum(sent_up.astype(jnp.float32), axis=0),
        ]
    )
    total = dequantize(grad_codes, grad_scales) + grads
    squared = by_axis(jnp.sum(total * total), OUTER_INNER)
    rms = jnp.sqrt(squared / (2.0 * D * FF) + 1e-06)
    update = total / rms
    return (hidden, input_grad, update)


def solution(mesh):
    finer = Mesh(
        mesh.devices.reshape(4, 8, 2, 4, 2), ("outer_0", "outer_1", "inner_0", "inner_1", "inner_2")
    )
    return jax.shard_map(
        local,
        mesh=finer,
        in_specs=(
            P(INNER, None),
            P(None, INNER, OUTER),
            P(None, INNER, OUTER),
            P(None, INNER, OUTER),
            P(None, INNER, OUTER),
            P(INNER, OUTER),
        ),
        out_specs=(P(INNER, OUTER), P(INNER, OUTER), P(None, INNER, OUTER)),
        check_vma=False,
    )
```

profile of v0, /device:TPU:1, one launch (start us, length us, event | category | flops | bytes accessed | tf_op | source)
XLA Modules:
  0.0 408.7 jit_solution(2064696816639945534)
XLA Ops:
  7.2 1.0 copy.12
  8.3 1.9 mul.49
  10.1 1.9 mul.50
  12.0 2.1 multiply_convert_fusion
  14.2 115.3 %all-gather.2.cloned.1.call-done = bf16[2,4096,448]{1,2,0:T(8,128)(2,1)} async-done(((bf16[2,256,448]{1,2,0:T(8,128)(2,1)}), bf16[2,4096,448]{1,2,0:T(8,128)(2,1)}) %all-gather.2.cloned.1.call-update) | async-done | bytes 7340048 | tf_op jit(solution)/shard_map/all_gather | solution.py:53
  129.5 3.2 fusion.6
  132.7 1.1 convolution_convert_fusion
  133.8 2.2 copy.22
  136.0 4.5 %all-to-all-start.1 = ((bf16[16,256,448]{1,2,0:T(8,128)(2,1)}), bf16[16,256,448]{1,2,0:T(8,128)(2,1)}, u32[]{:S(2)}, u32[]{:S(2)}) async-start(bf16[16,256,448]{1,2,0:T(8,128)(2,1)} %bitcast.56), calls=%async_computation.3 | async-start | bytes 7340032 | tf_op jit(solution)/shard_map/all_to_all | solution.py:77
  140.5 3.9 fusion.9
  144.4 1.1 convolution_convert_fusion.1
  145.6 2.3 copy.23
  147.9 46.4 %all-to-all-done.1 = bf16[16,256,448]{1,2,0:T(8,128)(2,1)} async-done(((bf16[16,256,448]{1,2,0:T(8,128)(2,1)}), bf16[16,256,448]{1,2,0:T(8,128)(2,1)}, u32[]{:S(2)}, u32[]{:S(2)}) %all-to-all-start.1) | async-done | bytes 3670048 | tf_op jit(solution)/shard_map/all_to_all | solution.py:77
  194.3 6.0 %all-to-all-start = ((bf16[16,256,448]{1,2,0:T(8,128)(2,1)}), bf16[16,256,448]{1,2,0:T(8,128)(2,1)}, u32[]{:S(2)}, u32[]{:S(2)}) async-start(bf16[16,256,448]{1,2,0:T(8,128)(2,1)} %bitcast.55), calls=%async_computation.2 | async-start | bytes 7340032 | tf_op jit(solution)/shard_map/all_to_all | solution.py:69
  200.4 3.3 fusion.1
  203.7 3.4 fusion.4
  207.1 0.5 copy.19
  207.6 2.2 copy.13
  209.8 0.2 reduce-scatter.5.cloned.1.call-start
  210.2 1.9 mul.60
  212.1 1.9 mul.61
  214.0 120.8 %reduce-scatter.3.cloned.1.call-done = bf16[4,256,128]{2,1,0:T(8,128)(2,1)} async-done(((bf16[32,256,128]{2,1,0:T(8,128)(2,1)}), bf16[4,256,128]{2,1,0:T(8,128)(2,1)}) %reduce-scatter.3.cloned.1.call-update) | async-done | bytes 262160 | tf_op jit(solution)/shard_map/reduce_scatter | solution.py:20
  334.9 2.6 convert_reduce_fusion
  337.5 2.7 convert_reduce_fusion.1
  340.2 0.8 copy-done.1
  340.9 0.9 multiply_reduce_fusion
  341.8 11.1 %psum.35 = f32[]{:T(128)} all-reduce(f32[]{:T(128)} %multiply_reduce_fusion), channel_id=1, replica_groups=mesh['outer_0'=4,'outer_1'=8,'inner_0'=2,'inner_1'=4,'inner_2'=2] {'oute..., use_global_device_ids=true, to_apply=%region_5.0 | all-reduce | flops 1 | bytes 8 | tf_op jit(solution)/shard_map/psum | solution.py:36
  352.8 13.5 %psum.36 = f32[]{:T(128)} all-reduce(f32[]{:T(128)} %psum.35), channel_id=1, replica_groups=mesh['outer_0'=4,'outer_1'=8,'inner_0'=2,'inner_1'=4,'inner_2'=2] {'oute..., use_global_device_ids=true, to_apply=%region_6.0 | all-reduce | flops 1 | bytes 8 | tf_op jit(solution)/shard_map/psum | solution.py:36
  366.3 8.3 %psum.37 = f32[]{:T(128)} all-reduce(f32[]{:T(128)} %psum.36), channel_id=1, replica_groups=mesh['outer_0'=4,'outer_1'=8,'inner_0'=2,'inner_1'=4,'inner_2'=2] {'inne..., use_global_device_ids=true, to_apply=%region_7.0 | all-reduce | flops 1 | bytes 8 | tf_op jit(solution)/shard_map/psum | solution.py:36
  374.6 12.4 %psum.38 = f32[]{:T(128)} all-reduce(f32[]{:T(128)} %psum.37), channel_id=1, replica_groups=mesh['outer_0'=4,'outer_1'=8,'inner_0'=2,'inner_1'=4,'inner_2'=2] {'inne..., use_global_device_ids=true, to_apply=%region_8.0 | all-reduce | flops 1 | bytes 8 | tf_op jit(solution)/shard_map/psum | solution.py:36
  387.0 12.0 %psum.39 = f32[]{:T(128)} all-reduce(f32[]{:T(128)} %psum.38), channel_id=1, replica_groups=mesh['outer_0'=4,'outer_1'=8,'inner_0'=2,'inner_1'=4,'inner_2'=2] {'inne..., use_global_device_ids=true, to_apply=%region_9.0 | all-reduce | flops 1 | bytes 8 | tf_op jit(solution)/shard_map/psum | solution.py:36
  399.7 2.4 broadcast_divide_fusion
  (17 shorter events, 0.4 us)
Async XLA Ops:
  7.2 122.3 %copy-start = (bf16[256,4096]{1,0:T(8,128)(2,1)S(1)}, bf16[256,4096]{1,0:T(8,128)(2,1)}, u32[]{:S(2)}) copy-start(bf16[256,4096]{1,0:T(8,128)(2,1)} %param.6) | copy-start | bytes 6291460
  7.2 122.3 %all-gather.2.cloned.1.call-start = ((), (), s32[]{:S(2)}) async-start(), calls=%async_computation.4 | async-start | bytes 7798784 | tf_op jit(solution)/shard_map/all_gather | solution.py:53
  14.1 118.5 %copy-start.3 = (bf16[256,448]{0,1:T(8,128)(2,1)S(1)}, bf16[256,448]{0,1:T(8,128)(2,1)}, u32[]{:S(2)}) copy-start(bf16[256,448]{0,1:T(8,128)(2,1)} %param.11) | copy-start | bytes 688132
  136.0 58.3 %all-to-all-start.1 = ((bf16[16,256,448]{1,2,0:T(8,128)(2,1)}), bf16[16,256,448]{1,2,0:T(8,128)(2,1)}, u32[]{:S(2)}, u32[]{:S(2)}) async-start(bf16[16,256,448]{1,2,0:T(8,128)(2,1)} %bitcast.56), calls=%async_computation.3 | async-start | bytes 7340032 | tf_op jit(solution)/shard_map/all_to_all | solution.py:77
  194.3 143.2 %all-to-all-start = ((bf16[16,256,448]{1,2,0:T(8,128)(2,1)}), bf16[16,256,448]{1,2,0:T(8,128)(2,1)}, u32[]{:S(2)}, u32[]{:S(2)}) async-start(bf16[16,256,448]{1,2,0:T(8,128)(2,1)} %bitcast.55), calls=%async_computation.2 | async-start | bytes 7340032 | tf_op jit(solution)/shard_map/all_to_all | solution.py:69
  200.3 134.5 %reduce-scatter.3.cloned.1.call-start = ((), (), s32[]{:S(2)}) async-start(), calls=%async_computation.5 | async-start | bytes 2359296 | tf_op jit(solution)/shard_map/reduce_scatter | solution.py:20
  207.6 2.4 copy-start.4
  209.8 192.4 %reduce-scatter.5.cloned.1.call-start = ((), (), s32[]{:S(2)}) async-start(), calls=%async_computation.6 | async-start | bytes 327680 | tf_op jit(solution)/shard_map/reduce_scatter | solution.py:20
  337.5 3.5 copy-start.2
  340.1 0.8 copy-start.1
Sparse Core Ops, SparseCore 0:
  14.3 115.1 all-gather.1
  209.9 124.9 reduce-scatter.2
  338.2 29.5 reduce-scatter.4
where the time goes:
time: 409 us
  waiting for transfers between devices  283 us (69%)
  blocking collectives  57.2 us (14%)
  local copies, waits for them, and re-layouts  16.7 us (4%)
  matrix products  16.1 us (4%)
  between operations  14.6 us (4%)
  starting transfers between devices  10.8 us (3%)
  other arithmetic  10.6 us (3%)
    reduce_scatter x2, waiting for transfers between devices, reduced_to_own(): blocks = lax.psum_scatter(blocks, axes[k], scatter_dimension=0, tiled=True)  121 us
    all_gather x1, waiting for transfers between devices, local(): whole = lax.all_gather(local_rows, INNER, axis=1, tiled=True)  115 us
    psum x5, blocking collectives, by_axis(): value = lax.psum(value, axis)  57.2 us
    all_to_all x1, waiting for transfers between devices, local(): lax.all_to_all(part_up.reshape((groups, part_up.shape[0] // groups, cols)...  46.4 us
  transfers between devices with their start and end apart: 5, of which 3 were waited for; matrix products, arithmetic and copies ran while one was open for 7% of the time, Pallas kernels for 0%

commit v1 on v0

v1 whole, which is shorter than its diff:
```python
import functools

import jax
import jax.numpy as jnp
from jax import lax
from jax.experimental import pallas as pl
from jax.experimental.pallas import tpu as pltpu
from jax.sharding import Mesh
from jax.sharding import PartitionSpec as P

D = 4096
FF = 14336
QBLOCK = 128
INNER = ("inner_0", "inner_1", "inner_2")
OUTER = ("outer_0", "outer_1")
ROWS = 256
COLS = 448
CAT = 2 * COLS
MESH = pl.DeviceIdType.MESH
F32 = jnp.float32
BF16 = jnp.bfloat16

PAIRS = ((0, 2, 0), (1, 3, 1), (4, 5, 2))
MIXED = 6

GATHER_SLOTS = {
    name: k
    for k, name in enumerate(
        [f"{b}{h}" for b in ("l", "r", "a") for h in range(2)]
        + [f"{b}{q}" for b in ("p", "pl", "pr", "pa") for q in range(4)]
    )
}
ROLES = ("own", "r", "l", "a", "p", "pr", "pl", "pa")


def tile(t):
    return slice(t * 128, (t + 1) * 128)


def wait_bytes(ref, sem):
    pltpu.make_async_copy(ref, ref, sem).wait()


class Gather:
    def __init__(self, at, buf, transit, send, recv, relay, sib):
        self.at, self.buf, self.transit = at, buf, transit
        self.send, self.recv, self.relay, self.sib = send, recv, relay, sib
        zh, x, c = at["zh"], at["x"], at["c"]

        def chip(h, k):
            return h * 4 + lax.rem(x + k, 4)

        other = 1 - zh
        self.chip = {
            "own": chip(zh, 0),
            "r": chip(zh, 1),
            "a": chip(zh, 2),
            "l": chip(zh, 3),
            "p": chip(other, 0),
            "pr": chip(other, 1),
            "pa": chip(other, 2),
            "pl": chip(other, 3),
        }

    def rows(self, role, first, count, sibling=False):
        c = self.at["c"]
        block = self.chip[role] * 2 + (1 - c if sibling else c)
        return self.buf.at[pl.ds(pl.multiple_of(block * ROWS + first, 64), count)]

    def copy(self, src, dst, recv, where):
        pltpu.make_async_remote_copy(
            src_ref=src,
            dst_ref=dst,
            send_sem=self.send,
            recv_sem=recv,
            device_id=where,
            device_id_type=MESH,
        ).start()

    def along_x(self, role, first, count, right, slot):
        part = self.rows(role, first, count)
        where = {"inner_1": self.at["right"] if right else self.at["left"]}
        self.copy(part, part, self.recv.at[GATHER_SLOTS[slot]], where)

    def along_z(self, q):
        part = self.rows("own", q * 64, 64)
        where = self.at["up2"] if q < 2 else self.at["down2"]
        self.copy(part, self.transit.at[q], self.relay.at[q], where)

    def pass_on(self, q):
        wait_bytes(self.transit.at[q], self.relay.at[q])
        at = self.at
        origin = at["down2"] if q < 2 else at["up2"]
        where = at["up2"] if q < 2 else at["down2"]
        block = (origin["inner_0"] * 4 + at["x"]) * 2 + at["c"]
        dst = self.buf.at[pl.ds(pl.multiple_of(block * ROWS + q * 64, 64), 64)]
        self.copy(self.transit.at[q], dst, self.recv.at[GATHER_SLOTS[f"p{q}"]], where)

    def to_sibling(self, role):
        part = self.rows(role, 0, ROWS)
        self.copy(part, part, self.sib.at[ROLES.index(role)], {"inner_2": 1 - self.at["c"]})

    def start(self):
        for q in (0, 2):
            self.along_z(q)
        self.along_x("own", 0, 128, True, "l0")
        self.along_x("own", 128, 128, False, "r1")
        for q in (1, 3):
            self.along_z(q)
        self.along_x("own", 128, 128, True, "l1")
        self.along_x("own", 0, 128, False, "r0")
        self.to_sibling("own")

    def wait_half(self, role, h):
        wait_bytes(self.rows(role, h * 128, 128), self.recv.at[GATHER_SLOTS[f"{role}{h}"]])

    def wait_quarter(self, role, q):
        wait_bytes(self.rows(role, q * 64, 64), self.recv.at[GATHER_SLOTS[f"{role}{q}"]])

    def first_hop(self):
        self.wait_half("l", 0)
        self.along_x("l", 0, 128, True, "a0")
        self.wait_half("r", 1)
        self.along_x("r", 128, 128, False, "a1")

    def near_done(self):
        self.wait_half("l", 1)
        self.to_sibling("l")
        self.wait_half("r", 0)
        self.to_sibling("r")

    def far_done(self):
        self.wait_half("a", 0)
        self.wait_half("a", 1)
        self.to_sibling("a")

    def partner(self, qs):
        for q in qs:
            self.wait_quarter("p", q)
            self.along_x("p", q * 64, 64, True, f"pl{q}")
            self.along_x("p", q * 64, 64, False, f"pr{q}")

    def partner_hop(self, up, down):
        self.wait_quarter("pl", up)
        self.along_x("pl", up * 64, 64, True, f"pa{up}")
        self.wait_quarter("pr", down)
        self.along_x("pr", down * 64, 64, False, f"pa{down}")

    def partner_near_done(self):
        for q in (2, 3):
            self.wait_quarter("pl", q)
        self.to_sibling("pl")
        for q in (0, 1):
            self.wait_quarter("pr", q)
        self.to_sibling("pr")

    def partner_far_done(self):
        for q in (0, 2, 1, 3):
            self.wait_quarter("pa", q)
        self.to_sibling("pa")

    def unit(self, role):
        wait_bytes(self.rows(role, 0, ROWS, True), self.sib.at[ROLES.index(role)])
        return pl.multiple_of(self.chip[role] * 512, 512)

    def finish(self):
        wait_bytes(self.buf, self.send)


def kernel(
    tok_h,
    wc_h,
    ws_h,
    gc_h,
    gs_h,
    cot_h,
    hid_o,
    ig_o,
    upd_o,
    tok,
    wc,
    ws,
    gc,
    gs,
    cot,
    wbuf,
    dbuf,
    wtransit,
    dtransit,
    xt,
    acc,
    term,
    landed,
    zsend,
    zland,
    igacc,
    hid,
    ig,
    upd,
    part,
    parts,
    load_sem,
    out_sem,
    wsend,
    wrecv,
    wrelay,
    wsib,
    dsend,
    drecv,
    drelay,
    dsib,
    xsend,
    xrecv,
    ysend,
    yrecv,
    rsend,
    rrecv,
    zs_send,
    zs_recv,
    msend,
    mrecv,
):
    zl, y = lax.axis_index("outer_0"), lax.axis_index("outer_1")
    zh, x, c = (lax.axis_index(a) for a in INNER)
    z = zh * 4 + zl
    me = (zh * 4 + x) * 2 + c

    def z_at(k):
        there = lax.rem(z + k, 8)
        return {"outer_0": lax.rem(there, 4), "inner_0": there // 4}

    def inner_at(k):
        there = lax.rem(me + k, 16)
        return there, {
            "inner_0": there // 8,
            "inner_1": lax.rem(there // 2, 4),
            "inner_2": lax.rem(there, 2),
        }

    def plane_at(k):
        there = lax.rem(x * 2 + c + k, 8)
        return {"inner_1": there // 2, "inner_2": lax.rem(there, 2)}

    def y_at(k):
        return {"outer_1": lax.rem(y + k, 8)}

    at = {
        "zh": zh,
        "x": x,
        "c": c,
        "right": lax.rem(x + 1, 4),
        "left": lax.rem(x + 3, 4),
        "up2": z_at(2),
        "down2": z_at(6),
    }

    barrier = pltpu.get_barrier_semaphore()
    greeted = [inner_at(k)[1] for k in range(1, 16)]
    greeted += [z_at(k) for k in (1, 2, 3, 5, 6, 7)]
    greeted += [y_at(k) for k in range(1, 8)]
    for where in greeted:
        pl.semaphore_signal(barrier, inc=1, device_id=where, device_id_type=MESH)

    loads = [
        pltpu.make_async_copy(src, dst, load_sem.at[k])
        for k, (src, dst) in enumerate(
            ((ws_h, ws), (wc_h, wc), (tok_h, tok), (cot_h, cot), (gs_h, gs), (gc_h, gc))
        )
    ]
    for load in loads:
        load.start()

    loads[0].wait()
    loads[1].wait()
    own_row = pl.multiple_of(me * ROWS, ROWS)

    def dequantize(i, carry, half):
        here = pl.ds(pl.multiple_of(half * QBLOCK + i * 32, 32), 32)
        there = pl.ds(pl.multiple_of(own_row + half * QBLOCK + i * 32, 32), 32)

        def value(k, lanes):
            return wc[k, here, lanes].astype(F32) * ws[k, half : half + 1, lanes]

        for g, u, t in PAIRS:
            wbuf[there, tile(g)] = value(0, tile(t)).astype(BF16)
            wbuf[there, tile(u)] = value(1, tile(t)).astype(BF16)
        last = slice(384, 448)
        mixed = jnp.concatenate([value(0, last), value(1, last)], axis=1)
        wbuf[there, tile(MIXED)] = mixed.astype(BF16)
        return carry

    for half in range(2):
        lax.fori_loop(0, QBLOCK // 32, functools.partial(dequantize, half=half), 0)
    loads[2].wait()
    pl.semaphore_wait(barrier, len(greeted))

    own_tokens = pl.ds(pl.multiple_of(y * 32, 32), 32)
    for k in range(1, 16):
        there, where = inner_at(k)
        pltpu.make_async_remote_copy(
            src_ref=tok.at[own_tokens, pl.ds(pl.multiple_of(there * ROWS, ROWS), ROWS)],
            dst_ref=xt.at[me, y],
            send_sem=xsend,
            recv_sem=xrecv,
            device_id=where,
            device_id_type=MESH,
        ).start()
    weights = Gather(at, wbuf, wtransit, wsend, wrecv, wrelay, wsib)
    weights.start()
    xt[me, y] = tok[own_tokens, pl.ds(pl.multiple_of(me * ROWS, ROWS), ROWS)]

    def y_share(k, right, slot):
        share = xt.at[:, lax.rem(y + k, 8)]
        pltpu.make_async_remote_copy(
            src_ref=share,
            dst_ref=share,
            send_sem=ysend,
            recv_sem=yrecv.at[slot],
            device_id=y_at(1 if right else 7),
            device_id_type=MESH,
        ).start()

    def y_wait(k, slot):
        wait_bytes(xt.at[:, lax.rem(y + k, 8)], yrecv.at[slot])

    def y_first():
        wait_bytes(xt.at[pl.ds(0, 15), 0], xrecv)
        y_share(0, True, 0)
        y_share(0, False, 4)

    def y_step(s):
        y_wait(8 - s, s - 1)
        if s < 4:
            y_share(8 - s, True, s)
        if s < 4:
            y_wait(s, 3 + s)
        if s < 3:
            y_share(s, False, 4 + s)

    def multiply(role, first=False):
        row = weights.unit(role)
        product = jnp.dot(
            tok[:, pl.ds(row, 512)], wbuf[pl.ds(row, 512), :], preferred_element_type=F32
        )
        acc[...] = product if first else acc[...] + product

    multiply("own", True)
    y_first()
    weights.first_hop()
    for q in (0, 2):
        weights.pass_on(q)
    weights.near_done()
    y_step(1)
    for q in (1, 3):
        weights.pass_on(q)
    weights.partner((0, 2))
    multiply("r")
    multiply("l")
    weights.far_done()
    y_step(2)
    multiply("a")
    weights.partner_hop(0, 2)
    weights.partner((1, 3))
    weights.to_sibling("p")
    weights.partner_hop(1, 3)
    weights.partner_near_done()
    y_step(3)
    multiply("p")
    weights.partner_far_done()
    multiply("pl")
    multiply("pr")
    multiply("pa")

    loads[3].wait()

    def activate(i, carry):
        here = pl.ds(pl.multiple_of(i * 32, 32), 32)
        there = pl.ds(pl.multiple_of(own_row + i * 32, 32), 32)

        def grads(gate, up, back):
            sig = jax.nn.sigmoid(gate)
            d_gate = back * up * sig * (1.0 + gate * (1.0 - sig))
            return gate * sig * up, d_gate, back * gate * sig

        for g, u, t in PAIRS:
            back = cot[here, tile(t)].astype(F32)
            value, d_gate, d_up = grads(acc[here, tile(g)], acc[here, tile(u)], back)
            hid[here, tile(t)] = value.astype(BF16)
            dbuf[there, tile(g)] = d_gate.astype(BF16)
            dbuf[there, tile(u)] = d_up.astype(BF16)
        last = slice(384, 448)
        mixed = acc[here, tile(MIXED)]
        back = cot[here, last].astype(F32)
        gate, up = mixed[:, :64], pltpu.roll(mixed, 64, 1)[:, :64]
        value, d_gate, d_up = grads(gate, up, back)
        hid[here, last] = value.astype(BF16)
        dbuf[there, tile(MIXED)] = jnp.concatenate([d_gate, d_up], axis=1).astype(BF16)
        return carry

    lax.fori_loop(0, ROWS // 32, activate, 0)

    deltas = Gather(at, dbuf, dtransit, dsend, drecv, drelay, dsib)
    deltas.start()
    hid_out = pltpu.make_async_copy(hid, hid_o, out_sem.at[0])
    hid_out.start()

    def partial_inputs(k):
        pair = lax.rem(lax.rem(y + 4, 8) // 2 + k, 4)
        own = dbuf[pl.ds(own_row, ROWS), :]
        for run in range(4):
            row = pl.multiple_of((run * 4 + pair) * ROWS, ROWS)
            product = lax.dot_general(
                own,
                wbuf[pl.ds(row, ROWS), :],
                (((1,), (1,)), ((), ())),
                preferred_element_type=F32,
            ).astype(BF16)
            term[pair * 2, run] = product[:, :128]
            term[pair * 2 + 1, run] = product[:, 128:]

    def target(d, s):
        return lax.rem(y + (4 - s if d == 0 else 4 + s), 8)

    def reduce_send(d, s, h):
        pltpu.make_async_remote_copy(
            src_ref=term.at[target(d, s), pl.ds(h * 2, 2)],
            dst_ref=landed.at[d, s, h],
            send_sem=rsend,
            recv_sem=rrecv.at[(d * 4 + s) * 2 + h],
            device_id=y_at(1 if d == 0 else 7),
            device_id_type=MESH,
        ).start()

    def reduce_wait(d, s, h):
        wait_bytes(landed.at[d, s, h], rrecv.at[(d * 4 + s) * 2 + h])

    def reduce_step(d, s, h):
        reduce_wait(d, s, h)
        goal = target(d, s + 1)

        def add(i, carry):
            here = pl.ds(pl.multiple_of(i * 64, 64), 64)
            for k in range(2):
                came = landed[d, s, h, k, here].astype(F32)
                mine = term[goal, h * 2 + k, here].astype(F32)
                term[goal, h * 2 + k, here] = (mine + came).astype(BF16)
            return carry

        lax.fori_loop(0, ROWS // 64, add, 0)
        reduce_send(d, s + 1, h)

    def reduce_last():
        for h in range(2):
            for d in range(2):
                reduce_wait(d, 3, h)
        for k in (1, 2, 3, 0):
            run = lax.rem(zl + k, 4)

            def add(i, carry, k=k, run=run):
                here = pl.ds(pl.multiple_of(i * 64, 64), 64)
                total = term[y, run, here].astype(F32)
                for d in range(2):
                    total = total + landed[d, 3, run // 2, lax.rem(run, 2), here].astype(F32)
                if k:
                    zsend[k - 1, here] = total.astype(BF16)
                else:
                    igacc[here] = total
                return carry

            lax.fori_loop(0, ROWS // 64, add, 0)
            if k:
                pltpu.make_async_remote_copy(
                    src_ref=zsend.at[k - 1],
                    dst_ref=zland.at[k - 1],
                    send_sem=zs_send,
                    recv_sem=zs_recv,
                    device_id={"outer_0": run},
                    device_id_type=MESH,
                ).start()

    def input_done():
        wait_bytes(zland, zs_recv)

        def add(i, carry):
            here = pl.ds(pl.multiple_of(i * 64, 64), 64)
            total = igacc[here]
            for k in range(3):
                total = total + zland[k, here].astype(F32)
            ig[here] = total.astype(BF16)
            return carry

        lax.fori_loop(0, ROWS // 64, add, 0)

    def accumulate(role, first=False):
        row = deltas.unit(role)
        block = xt[pl.ds(pl.multiple_of(deltas.chip[role] * 2, 2), 2)].reshape(512, ROWS)
        product = lax.dot_general(
            block,
            dbuf[pl.ds(row, 512), :],
            (((0,), (0,)), ((), ())),
            preferred_element_type=F32,
        )
        acc[...] = product if first else acc[...] + product

    partial_inputs(0)
    reduce_send(0, 0, 0)
    reduce_send(1, 0, 1)
    partial_inputs(1)
    partial_inputs(3)
    reduce_send(0, 1, 1)
    reduce_send(1, 1, 0)
    partial_inputs(2)
    y_step(4)
    accumulate("own", True)
    deltas.first_hop()
    reduce_step(0, 0, 0)
    reduce_step(1, 0, 1)
    for q in (0, 2):
        deltas.pass_on(q)
    reduce_step(0, 1, 1)
    reduce_step(1, 1, 0)
    deltas.near_done()
    reduce_step(0, 1, 0)
    reduce_step(1, 1, 1)
    for q in (1, 3):
        deltas.pass_on(q)
    deltas.partner((0, 2))
    reduce_step(0, 2, 1)
    reduce_step(1, 2, 0)
    accumulate("r")
    accumulate("l")
    deltas.far_done()
    reduce_step(0, 2, 0)
    reduce_step(1, 2, 1)
    deltas.partner_hop(0, 2)
    deltas.partner((1, 3))
    deltas.to_sibling("p")
    reduce_last()
    accumulate("a")
    deltas.partner_hop(1, 3)
    deltas.partner_near_done()
    accumulate("p")
    input_done()
    ig_out = pltpu.make_async_copy(ig, ig_o, out_sem.at[1])
    ig_out.start()
    deltas.partner_far_done()
    accumulate("pl")
    accumulate("pr")
    accumulate("pa")

    loads[4].wait()
    loads[5].wait()

    def totals(i, carry, half):
        wide, narrow = carry
        here = pl.ds(pl.multiple_of(half * QBLOCK + i * 32, 32), 32)

        def add(k, lanes, grad):
            total = gc[k, here, lanes].astype(F32) * gs[k, half : half + 1, lanes] + grad
            upd[k, here, lanes] = total
            return jnp.sum((total * total).reshape(4, 8, total.shape[1]), axis=0)

        for g, u, t in PAIRS:
            wide = wide + add(0, tile(t), acc[here, tile(g)])
            wide = wide + add(1, tile(t), acc[here, tile(u)])
        last = slice(384, 448)
        mixed = acc[here, tile(MIXED)]
        narrow = narrow + add(0, last, mixed[:, :64])
        narrow = narrow + add(1, last, pltpu.roll(mixed, 64, 1)[:, :64])
        return wide, narrow

    squares = (jnp.zeros((8, 128), F32), jnp.zeros((8, 64), F32))
    for half in range(2):
        squares = lax.fori_loop(0, QBLOCK // 32, functools.partial(totals, half=half), squares)
    wide, narrow = squares
    part[0] = jnp.broadcast_to(
        jnp.sum(wide, keepdims=True) + jnp.sum(narrow, keepdims=True), (8, 128)
    )
    value = part[0]
    for stage, peer in enumerate((plane_at, z_at, y_at)):
        for k in range(1, 8):
            pltpu.make_async_remote_copy(
                src_ref=part.at[stage],
                dst_ref=parts.at[stage, k - 1],
                send_sem=msend.at[stage],
                recv_sem=mrecv.at[stage],
                device_id=peer(k),
                device_id_type=MESH,
            ).start()
        wait_bytes(parts.at[stage], mrecv.at[stage])
        for k in range(7):
            value = value + parts[stage, k]
        if stage < 2:
            part[stage + 1] = value
    scale = 1.0 / jnp.sqrt(value / (2.0 * D * FF) + 1e-06)
    scale = scale[0:1, 0:1]

    outs = []
    for half in range(2):

        def normalize(i, carry, half=half):
            here = pl.ds(pl.multiple_of(half * 128 + i * 32, 32), 32)
            for k in range(2):
                upd[k, here, :] = upd[k, here, :] * scale
            return carry

        lax.fori_loop(0, 4, normalize, 0)
        rows = pl.ds(half * 128, 128)
        out = pltpu.make_async_copy(upd.at[:, rows], upd_o.at[:, rows], out_sem.at[2 + half])
        out.start()
        outs.append(out)

    weights.finish()
    deltas.finish()
    wait_bytes(xt.at[pl.ds(0, 15), 0], xsend)
    wait_bytes(xt.at[:, pl.ds(0, 7)], ysend)
    wait_bytes(term.at[pl.ds(0, 7)], rsend)
    wait_bytes(zsend, zs_send)
    for stage in range(3):
        wait_bytes(parts.at[stage], msend.at[stage])
    hid_out.wait()
    ig_out.wait()
    for out in outs:
        out.wait()


def local(tokens, weight_codes, weight_scales, grad_codes, grad_scales, cotangent):
    dma = pltpu.SemaphoreType.DMA
    slots = len(GATHER_SLOTS)
    gather = [dma, dma((slots,)), dma((4,)), dma((8,))]
    call = pl.pallas_call(
        kernel,
        out_shape=(
            jax.ShapeDtypeStruct((ROWS, COLS), BF16),
            jax.ShapeDtypeStruct((ROWS, 128), BF16),
            jax.ShapeDtypeStruct((2, ROWS, COLS), F32),
        ),
        in_specs=[pl.BlockSpec(memory_space=pl.ANY)] * 6,
        out_specs=[pl.BlockSpec(memory_space=pl.ANY)] * 3,
        scratch_shapes=[
            pltpu.VMEM((ROWS, D), BF16),
            pltpu.VMEM((2, ROWS, COLS), jnp.int32),
            pltpu.VMEM((2, 2, COLS), F32),
            pltpu.VMEM((2, ROWS, COLS), jnp.int32),
            pltpu.VMEM((2, 2, COLS), F32),
            pltpu.VMEM((ROWS, COLS), BF16),
            pltpu.VMEM((16 * ROWS, CAT), BF16),
            pltpu.VMEM((16 * ROWS, CAT), BF16),
            pltpu.VMEM((4, 64, CAT), BF16),
            pltpu.VMEM((4, 64, CAT), BF16),
            pltpu.VMEM((16, 8, 32, ROWS), BF16),
            pltpu.VMEM((ROWS, CAT), F32),
            pltpu.VMEM((8, 4, ROWS, 128), BF16),
            pltpu.VMEM((2, 4, 2, 2, ROWS, 128), BF16),
            pltpu.VMEM((3, ROWS, 128), BF16),
            pltpu.VMEM((3, ROWS, 128), BF16),
            pltpu.VMEM((ROWS, 128), F32),
            pltpu.VMEM((ROWS, COLS), BF16),
            pltpu.VMEM((ROWS, 128), BF16),
            pltpu.VMEM((2, ROWS, COLS), F32),
            pltpu.VMEM((3, 8, 128), F32),
            pltpu.VMEM((3, 7, 8, 128), F32),
            dma((6,)),
            dma((4,)),
            *gather,
            *gather,
            dma,
            dma,
            dma,
            dma((7,)),
            dma,
            dma((16,)),
            dma,
            dma,
            dma((3,)),
            dma((3,)),
        ],
        compiler_params=pltpu.CompilerParams(
            collective_id=0, has_side_effects=True, vmem_limit_bytes=60 * 1024 * 1024
        ),
    )
    return tuple(
        call(tokens, weight_codes, weight_scales, grad_codes, grad_scales, cotangent)
    )


def solution(mesh):
    finer = Mesh(
        mesh.devices.reshape(4, 8, 2, 4, 2), ("outer_0", "outer_1", "inner_0", "inner_1", "inner_2")
    )
    return jax.shard_map(
        local,
        mesh=finer,
        in_specs=(
            P(INNER, None),
            P(None, INNER, OUTER),
            P(None, INNER, OUTER),
            P(None, INNER, OUTER),
            P(None, INNER, OUTER),
            P(INNER, OUTER),
        ),
        out_specs=(P(INNER, OUTER), P(INNER, OUTER), P(None, INNER, OUTER)),
        check_vma=False,
    )
```

time: 409 us -> 130 us (0.32)
  waiting for transfers between devices: 283 us -> 0 us
  Pallas kernels: 0 us -> 119 us
  blocking collectives: 57.2 us -> 0 us
  matrix products: 16.1 us -> 0 us
  between operations: 14.6 us -> 0.66 us
  starting transfers between devices: 10.8 us -> 0 us
  other arithmetic: 10.6 us -> 0 us
  local copies, waits for them, and re-layouts: 16.7 us -> 10.6 us
    reduce_scatter x2 -> x0, waiting for transfers between devices: 121 us -> none  [reduced_to_own(): blocks = lax.psum_scatter(blocks, axes[k], scatter_dimension=0, tiled=True)]
    pallas_call x0 -> x1, Pallas kernels: none -> 119 us  [local(): call(tokens, weight_codes, weight_scales, grad_codes, grad_scales, cotang...]
    all_gather x1 -> x0, waiting for transfers between devices: 115 us -> none  [local(): whole = lax.all_gather(local_rows, INNER, axis=1, tiled=True)]
    psum x5 -> x0, blocking collectives: 57.2 us -> none  [by_axis(): value = lax.psum(value, axis)]
    all_to_all x2 -> x0, waiting for transfers between devices: 46.4 us -> none  [the longest x1 46.4 us: local(): lax.all_to_all(part_up.reshape((groups, part_up.shape[0] // groups, cols)...]
    dot_general x6 -> x0, matrix products: 16.1 us -> none  [the longest x1 3.93 us: local(): up = jnp.dot(tokens, whole[1], preferred_element_type=jnp.float32)]
    all_to_all x2 -> x0, starting transfers between devices: 10.5 us -> none  [the longest x1 6.04 us: local(): lax.all_to_all(part_gate.reshape((groups, part_gate.shape[0] // groups, c...]
    mul x4 -> x0, local copies, waits for them, and re-layouts: 7.55 us -> none  [dequantize(): codes.reshape(count, rows // QBLOCK, QBLOCK, cols).astype(jnp.float32)]
  transfers between devices with their start and end apart: 5 -> 0, of which waited for: 3 -> 0; matrix products, arithmetic and copies ran while one was open for 7% -> 0% of each run, Pallas kernels for 0% -> 0%
where the time goes in v1:
time: 130 us
  Pallas kernels  119 us (92%)
  local copies, waits for them, and re-layouts  10.6 us (8%)
    pallas_call x1, Pallas kernels, local(): call(tokens, weight_codes, weight_scales, grad_codes, grad_scales, cotang...  119 us
    unnamed x8, local copies, waits for them, and re-layouts  6.34 us
    pallas_call x2, local copies, waits for them, and re-layouts, local(): call(tokens, weight_codes, weight_scales, grad_codes, grad_scales, cotang...  4.27 us

profile of v1, /device:TPU:1, one launch (start us, length us, event | category | flops | bytes accessed | tf_op | source)
XLA Modules:
  0.0 129.8 jit_solution(7464795850017909990)
XLA Ops:
  0.6 0.0 copy-start
  0.6 1.9 %copy.11.cot_h = bf16[256,448]{1,0:T(8,128)(2,1)} copy(bf16[256,448]{0,1:T(8,128)(2,1)} %param.11) | data formatting | bytes 458752 | tf_op args[5]
  2.5 2.5 %copy.9.wc_h = s32[2,256,448]{2,1,0:T(8,128)} copy(s32[2,256,448]{1,2,0:T(8,128)} %param.7) | data formatting | bytes 1835008 | tf_op args[1]
  5.0 0.0 copy-done
  5.0 1.4 %copy.10.gc_h = s32[2,256,448]{2,1,0:T(8,128)} copy(s32[2,256,448]{1,2,0:T(8,128)S(1)} %copy-done) | data formatting | bytes 1835008 | tf_op args[3]
  6.3 118.5 %shard_map.85 = (bf16[256,448]{1,0:T(8,128)(2,1)}, bf16[256,128]{1,0:T(8,128)(2,1)}, f32[2,256,448]{2,1,0:T(8,128)}) custom-call(bf16[256,4096]{1,0:T(8,128)(2,1)} %tok_h.1, s32[2,256,448]{2,1,0:T(8,128)} %copy.9.wc_h, f32[2,2,448]{2,1,0:T(2,128)} %ws_h.1, s32[2,256,448]{2,1,0:T(8,128)} %copy.10.gc_h, f32[2,2,448]{2,1,0:T(2,128)} %gs_h.1, ...), custom_call_target="tpu_custom_call" | custom-call | tf_op jit(solution)/shard_map/pallas_call | solution.py:683
  124.9 0.0 copy-start.1
  124.9 1.8 %copy.12 = bf16[256,448]{0,1:T(8,128)(2,1)} copy(bf16[256,448]{1,0:T(8,128)(2,1)} %get-tuple-element.3) | data formatting | bytes 458752 | tf_op jit(solution)/shard_map/pallas_call | solution.py:683
  126.7 2.5 %copy.13 = f32[2,256,448]{1,2,0:T(8,128)} copy(f32[2,256,448]{2,1,0:T(8,128)} %get-tuple-element.5) | data formatting | bytes 1835008 | tf_op jit(solution)/shard_map/pallas_call | solution.py:683
  129.2 0.0 copy-done.1
  129.2 0.6 copy.15
Async XLA Ops:
  0.6 4.4 %copy-start = (s32[2,256,448]{1,2,0:T(8,128)S(1)}, s32[2,256,448]{1,2,0:T(8,128)}, u32[]{:S(2)}) copy-start(s32[2,256,448]{1,2,0:T(8,128)} %param.9) | copy-start | bytes 2752516
  124.9 4.3 %copy-start.1 = (bf16[256,128]{1,0:T(8,128)(2,1)S(1)}, bf16[256,128]{1,0:T(8,128)(2,1)}, u32[]{:S(2)}) copy-start(bf16[256,128]{1,0:T(8,128)(2,1)} %get-tuple-element.10) | copy-start | bytes 196612

commit v2 on v1

v2 whole, which is shorter than its diff:
```python
import jax
import jax.numpy as jnp
from jax import lax
from jax.experimental import pallas as pl
from jax.experimental.pallas import tpu as pltpu
from jax.sharding import Mesh
from jax.sharding import PartitionSpec as P

D = 4096
FF = 14336
QBLOCK = 128
INNER = ("inner_0", "inner_1", "inner_2")
OUTER = ("outer_0", "outer_1")
ROWS = 256
COLS = 448
CAT = 2 * COLS
MESH = pl.DeviceIdType.MESH
F32 = jnp.float32
BF16 = jnp.bfloat16

HALF = COLS
PIECE = COLS // 4

GATHER_SLOTS = {
    name: k
    for k, name in enumerate(
        [f"{b}{h}" for b in ("l", "r", "a") for h in range(2)]
        + [f"{b}{q}" for b in ("p", "pl", "pr", "pa") for q in range(8)]
    )
}
ROLES = ("own", "r", "l", "a", "p", "pr", "pl", "pa")


def wait_bytes(ref, sem):
    pltpu.make_async_copy(ref, ref, sem).wait()


class Gather:
    def __init__(self, at, buf, transit, send, recv, relay, sib):
        self.at, self.buf, self.transit = at, buf, transit
        self.send, self.recv, self.relay, self.sib = send, recv, relay, sib
        zh, x, c = at["zh"], at["x"], at["c"]

        def chip(h, k):
            return h * 4 + lax.rem(x + k, 4)

        other = 1 - zh
        self.chip = {
            "own": chip(zh, 0),
            "r": chip(zh, 1),
            "a": chip(zh, 2),
            "l": chip(zh, 3),
            "p": chip(other, 0),
            "pr": chip(other, 1),
            "pa": chip(other, 2),
            "pl": chip(other, 3),
        }

    def rows(self, role, first, count, sibling=False):
        c = self.at["c"]
        block = self.chip[role] * 2 + (1 - c if sibling else c)
        return self.buf.at[pl.ds(pl.multiple_of(block * CAT + first, 16), count)]

    def piece(self, role, q):
        return self.rows(role, q * PIECE, PIECE)

    def copy(self, src, dst, recv, where):
        pltpu.make_async_remote_copy(
            src_ref=src,
            dst_ref=dst,
            send_sem=self.send,
            recv_sem=recv,
            device_id=where,
            device_id_type=MESH,
        ).start()

    def along_x(self, part, right, slot):
        where = {"inner_1": self.at["right"] if right else self.at["left"]}
        self.copy(part, part, self.recv.at[GATHER_SLOTS[slot]], where)

    def half(self, role, h):
        return self.rows(role, h * HALF, HALF)

    def along_z(self, q):
        where = self.at["up2"] if q < 4 else self.at["down2"]
        self.copy(self.piece("own", q), self.transit.at[q], self.relay.at[q], where)

    def pass_on(self, k):
        at = self.at
        for q in (k, k + 4):
            wait_bytes(self.transit.at[q], self.relay.at[q])
            origin = at["down2"] if q < 4 else at["up2"]
            where = at["up2"] if q < 4 else at["down2"]
            block = (origin["inner_0"] * 4 + at["x"]) * 2 + at["c"]
            dst = self.buf.at[pl.ds(pl.multiple_of(block * CAT + q * PIECE, 16), PIECE)]
            self.copy(self.transit.at[q], dst, self.recv.at[GATHER_SLOTS[f"p{q}"]], where)

    def to_sibling(self, role):
        part = self.rows(role, 0, CAT)
        self.copy(part, part, self.sib.at[ROLES.index(role)], {"inner_2": 1 - self.at["c"]})

    def start_z(self, ks):
        for k in ks:
            self.along_z(k)
            self.along_z(k + 4)

    def start_x(self):
        self.along_x(self.half("own", 0), True, "l0")
        self.along_x(self.half("own", 1), False, "r1")
        self.along_x(self.half("own", 1), True, "l1")
        self.along_x(self.half("own", 0), False, "r0")
        self.to_sibling("own")

    def wait_half(self, role, h):
        wait_bytes(self.half(role, h), self.recv.at[GATHER_SLOTS[f"{role}{h}"]])

    def wait_piece(self, role, q):
        wait_bytes(self.piece(role, q), self.recv.at[GATHER_SLOTS[f"{role}{q}"]])

    def first_hop(self):
        self.wait_half("l", 0)
        self.along_x(self.half("l", 0), True, "a0")
        self.wait_half("r", 1)
        self.along_x(self.half("r", 1), False, "a1")

    def near_done(self):
        self.wait_half("l", 1)
        self.to_sibling("l")
        self.wait_half("r", 0)
        self.to_sibling("r")

    def far_done(self):
        self.wait_half("a", 0)
        self.wait_half("a", 1)
        self.to_sibling("a")

    def partner(self, k):
        for q in (k, k + 4):
            self.wait_piece("p", q)
            self.along_x(self.piece("p", q), True, f"pl{q}")
            self.along_x(self.piece("p", q), False, f"pr{q}")
        if k == 3:
            self.to_sibling("p")

    def partner_hop(self, k):
        self.wait_piece("pl", k)
        self.along_x(self.piece("pl", k), True, f"pa{k}")
        self.wait_piece("pr", k + 4)
        self.along_x(self.piece("pr", k + 4), False, f"pa{k + 4}")

    def partner_near_done(self):
        for q in range(4, 8):
            self.wait_piece("pl", q)
        self.to_sibling("pl")
        for q in range(4):
            self.wait_piece("pr", q)
        self.to_sibling("pr")

    def partner_far_done(self):
        for k in range(4):
            self.wait_piece("pa", k)
            self.wait_piece("pa", k + 4)
        self.to_sibling("pa")

    def blocks(self, role):
        c = self.at["c"]
        for k, which in enumerate((c, 1 - c)):
            if k:
                wait_bytes(self.rows(role, 0, CAT, True), self.sib.at[ROLES.index(role)])
            number = self.chip[role] * 2 + which
            yield number, self.block(number)

    def block(self, number):
        return self.buf[pl.ds(pl.multiple_of(number * CAT, CAT), CAT), :]

    def finish(self):
        wait_bytes(self.buf, self.send)


def kernel(
    tok_h,
    wc_h,
    ws_h,
    gc_h,
    gs_h,
    cot_h,
    hid,
    ig,
    upd,
    scale,
    tok,
    wc,
    ws,
    gc,
    gs,
    cot,
    wbuf,
    dbuf,
    wtransit,
    dtransit,
    xt,
    acc,
    term,
    landed,
    zsend,
    zland,
    igacc,
    own,
    lanes,
    column,
    part,
    parts,
    load_sem,
    wsend,
    wrecv,
    wrelay,
    wsib,
    dsend,
    drecv,
    drelay,
    dsib,
    xsend,
    xrecv,
    ysend,
    yrecv,
    rsend,
    rrecv,
    zs_send,
    zs_recv,
    msend,
    mrecv,
):
    zl, y = lax.axis_index("outer_0"), lax.axis_index("outer_1")
    zh, x, c = (lax.axis_index(a) for a in INNER)
    z = zh * 4 + zl
    me = (zh * 4 + x) * 2 + c

    def z_at(k):
        there = lax.rem(z + k, 8)
        return {"outer_0": lax.rem(there, 4), "inner_0": there // 4}

    def inner_at(k):
        there = lax.rem(me + k, 16)
        return there, {
            "inner_0": there // 8,
            "inner_1": lax.rem(there // 2, 4),
            "inner_2": lax.rem(there, 2),
        }

    def plane_at(k):
        there = lax.rem(x * 2 + c + k, 8)
        return {"inner_1": there // 2, "inner_2": lax.rem(there, 2)}

    def y_at(k):
        return {"outer_1": lax.rem(y + k, 8)}

    at = {
        "zh": zh,
        "x": x,
        "c": c,
        "right": lax.rem(x + 1, 4),
        "left": lax.rem(x + 3, 4),
        "up2": z_at(2),
        "down2": z_at(6),
    }

    loads = [
        pltpu.make_async_copy(src, dst, load_sem.at[k])
        for k, (src, dst) in enumerate(
            ((ws_h, ws), (wc_h, wc), (tok_h, tok), (cot_h, cot), (gs_h, gs), (gc_h, gc))
        )
    ]
    for load in loads:
        load.start()

    barrier = pltpu.get_barrier_semaphore()
    greeted = [inner_at(k)[1] for k in range(1, 16)]
    greeted += [z_at(k) for k in (1, 2, 3, 5, 6, 7)]
    greeted += [y_at(k) for k in range(1, 8)]
    for where in greeted:
        pl.semaphore_signal(barrier, inc=1, device_id=where, device_id_type=MESH)

    loads[0].wait()
    loads[1].wait()
    own_row = pl.multiple_of(me * CAT, CAT)

    def columns(scales):
        for k in range(2):
            for g in range(2):
                lanes[2 * k + g : 2 * k + g + 1, 0:COLS] = scales[k, g : g + 1, :]
        column[...] = jnp.transpose(lanes[...])

    def scaled(codes, k, here):
        parts = [
            codes[k, here, g * QBLOCK : (g + 1) * QBLOCK].astype(F32)
            * column[here, 2 * k + g : 2 * k + g + 1]
            for g in range(2)
        ]
        return jnp.concatenate(parts, axis=1)

    columns(ws)

    def dequantize(first):
        def some(i, carry):
            here = pl.ds(pl.multiple_of(first * 32 + i * 32, 32), 32)
            for k in range(2):
                there = pl.ds(pl.multiple_of(own_row + k * COLS + first * 32 + i * 32, 32), 32)
                wbuf[there, :] = scaled(wc, k, here).astype(BF16)
            return carry

        lax.fori_loop(0, COLS // 64, some, 0)

    weights = Gather(at, wbuf, wtransit, wsend, wrecv, wrelay, wsib)
    dequantize(0)
    pl.semaphore_wait(barrier, len(greeted))
    weights.start_z((0, 1))
    dequantize(COLS // 64)
    weights.start_z((2, 3))
    loads[2].wait()

    own_tokens = pl.ds(pl.multiple_of(y * 32, 32), 32)

    def exchange_tokens(plane):
        for k in range(0 if plane else 1, 8):
            spot = lax.rem(x * 2 + c + k, 8)
            there = (1 - zh if plane else zh) * 8 + spot
            where = {
                "inner_0": there // 8,
                "inner_1": lax.rem(there // 2, 4),
                "inner_2": lax.rem(there, 2),
            }
            pltpu.make_async_remote_copy(
                src_ref=tok.at[own_tokens, pl.ds(pl.multiple_of(there * ROWS, ROWS), ROWS)],
                dst_ref=xt.at[me, y],
                send_sem=xsend.at[plane],
                recv_sem=xrecv.at[plane],
                device_id=where,
                device_id_type=MESH,
            ).start()

    exchange_tokens(0)
    weights.start_x()
    xt[me, y] = tok[own_tokens, pl.ds(pl.multiple_of(me * ROWS, ROWS), ROWS)]

    def share_of(k, plane):
        first = pl.multiple_of((1 - zh if plane else zh) * 8, 8)
        return xt.at[pl.ds(first, 8), lax.rem(y + k, 8)]

    def y_share(k, right, slot, plane):
        share = share_of(k, plane)
        pltpu.make_async_remote_copy(
            src_ref=share,
            dst_ref=share,
            send_sem=ysend,
            recv_sem=yrecv.at[plane * 7 + slot],
            device_id=y_at(1 if right else 7),
            device_id_type=MESH,
        ).start()

    def y_wait(k, slot, plane):
        wait_bytes(share_of(k, plane), yrecv.at[plane * 7 + slot])

    def y_first(plane):
        wait_bytes(xt.at[pl.ds(0, 7 + plane), 0], xrecv.at[plane])
        y_share(0, True, 0, plane)
        y_share(0, False, 4, plane)

    def y_step(s, plane):
        y_wait(8 - s, s - 1, plane)
        if s < 4:
            y_share(8 - s, True, s, plane)
        if s < 4:
            y_wait(s, 3 + s, plane)
        if s < 3:
            y_share(s, False, 4 + s, plane)

    def multiply(role):
        for k, (number, block) in enumerate(weights.blocks(role)):
            mine = tok[:, pl.ds(pl.multiple_of(number * ROWS, ROWS), ROWS)]
            product = lax.dot_general(
                block, mine, (((1,), (1,)), ((), ())), preferred_element_type=F32
            )
            acc[...] = product if role == "own" and k == 0 else acc[...] + product

    multiply("own")
    weights.pass_on(0)
    weights.first_hop()
    weights.pass_on(1)
    weights.pass_on(2)
    weights.near_done()
    exchange_tokens(1)
    weights.pass_on(3)
    y_first(0)
    weights.partner(0)
    multiply("r")
    multiply("l")
    weights.far_done()
    weights.partner(1)
    y_step(1, 0)
    weights.partner_hop(0)
    weights.partner(2)
    multiply("a")
    weights.partner(3)
    weights.partner_hop(1)
    y_step(2, 0)
    y_first(1)
    weights.partner_hop(2)
    multiply("p")
    y_step(3, 0)
    y_step(1, 1)
    weights.partner_hop(3)
    weights.partner_near_done()
    multiply("pl")
    multiply("pr")
    weights.partner_far_done()
    y_step(4, 0)
    multiply("pa")

    loads[3].wait()

    def activate(i, carry):
        here = pl.ds(pl.multiple_of(i * 32, 32), 32)
        gate = acc[here, :]
        up = acc[pl.ds(pl.multiple_of(COLS + i * 32, 32), 32), :]
        back = cot[here, :].astype(F32)
        sig = jax.nn.sigmoid(gate)
        d_gate = back * up * sig * (1.0 + gate * (1.0 - sig))
        d_up = back * gate * sig
        hid[here, :] = (gate * sig * up).astype(BF16)
        for k, value in enumerate((d_gate, d_up)):
            there = pl.ds(pl.multiple_of(own_row + k * COLS + i * 32, 32), 32)
            dbuf[there, :] = value.astype(BF16)
        return carry

    lax.fori_loop(0, COLS // 32, activate, 0)

    deltas = Gather(at, dbuf, dtransit, dsend, drecv, drelay, dsib)
    deltas.start_z(range(4))
    deltas.start_x()

    def partial_inputs(k):
        pair = lax.rem(lax.rem(y + 4, 8) // 2 + k, 4)
        for run in range(4):
            product = jnp.dot(
                own[...], weights.block(run * 4 + pair), preferred_element_type=F32
            ).astype(BF16)
            term[pair * 2, run] = product[:, :128]
            term[pair * 2 + 1, run] = product[:, 128:]

    def target(d, s):
        return lax.rem(y + (4 - s if d == 0 else 4 + s), 8)

    def reduce_send(d, s, h):
        pltpu.make_async_remote_copy(
            src_ref=term.at[target(d, s), pl.ds(h * 2, 2)],
            dst_ref=landed.at[d, s, h],
            send_sem=rsend,
            recv_sem=rrecv.at[(d * 4 + s) * 2 + h],
            device_id=y_at(1 if d == 0 else 7),
            device_id_type=MESH,
        ).start()

    def reduce_wait(d, s, h):
        wait_bytes(landed.at[d, s, h], rrecv.at[(d * 4 + s) * 2 + h])

    def reduce_step(d, s, h):
        reduce_wait(d, s, h)
        goal = target(d, s + 1)

        def add(i, carry):
            here = pl.ds(pl.multiple_of(i * 64, 64), 64)
            for k in range(2):
                came = landed[d, s, h, k, here].astype(F32)
                mine = term[goal, h * 2 + k, here].astype(F32)
                term[goal, h * 2 + k, here] = (mine + came).astype(BF16)
            return carry

        lax.fori_loop(0, ROWS // 64, add, 0)
        reduce_send(d, s + 1, h)

    def reduce_last():
        for h in range(2):
            for d in range(2):
                reduce_wait(d, 3, h)
        for k in (1, 2, 3, 0):
            run = lax.rem(zl + k, 4)

            def add(i, carry, k=k, run=run):
                here = pl.ds(pl.multiple_of(i * 64, 64), 64)
                total = term[y, run, here].astype(F32)
                for d in range(2):
                    total = total + landed[d, 3, run // 2, lax.rem(run, 2), here].astype(F32)
                if k:
                    zsend[k - 1, here] = total.astype(BF16)
                else:
                    igacc[here] = total
                return carry

            lax.fori_loop(0, ROWS // 64, add, 0)
            if k:
                pltpu.make_async_remote_copy(
                    src_ref=zsend.at[k - 1],
                    dst_ref=zland.at[k - 1],
                    send_sem=zs_send,
                    recv_sem=zs_recv,
                    device_id={"outer_0": run},
                    device_id_type=MESH,
                ).start()

    def input_done():
        wait_bytes(zland, zs_recv)

        def add(i, carry):
            here = pl.ds(pl.multiple_of(i * 64, 64), 64)
            total = igacc[here]
            for k in range(3):
                total = total + zland[k, here].astype(F32)
            ig[here] = total.astype(BF16)
            return carry

        lax.fori_loop(0, ROWS // 64, add, 0)

    def accumulate(role):
        for k, (number, block) in enumerate(deltas.blocks(role)):
            product = jnp.dot(
                block, xt[number].reshape(ROWS, ROWS), preferred_element_type=F32
            )
            acc[...] = product if role == "own" and k == 0 else acc[...] + product

    for t in range(CAT // 128):
        there = pl.ds(pl.multiple_of(own_row + t * 128, 128), 128)
        own[:, t * 128 : (t + 1) * 128] = jnp.transpose(dbuf[there, :])
    partial_inputs(0)
    reduce_send(0, 0, 0)
    reduce_send(1, 0, 1)
    partial_inputs(1)
    partial_inputs(3)
    reduce_send(0, 1, 1)
    reduce_send(1, 1, 0)
    y_step(2, 1)
    partial_inputs(2)
    deltas.pass_on(0)
    reduce_step(0, 0, 0)
    reduce_step(1, 0, 1)
    deltas.first_hop()
    deltas.pass_on(1)
    reduce_step(0, 1, 1)
    reduce_step(1, 1, 0)
    deltas.pass_on(2)
    deltas.near_done()
    deltas.pass_on(3)
    y_step(3, 1)
    reduce_step(0, 1, 0)
    reduce_step(1, 1, 1)
    accumulate("own")
    deltas.partner(0)
    reduce_step(0, 2, 1)
    reduce_step(1, 2, 0)
    accumulate("r")
    deltas.far_done()
    deltas.partner(1)
    accumulate("l")
    deltas.partner_hop(0)
    reduce_step(0, 2, 0)
    reduce_step(1, 2, 1)
    deltas.partner(2)
    deltas.partner_hop(1)
    deltas.partner(3)
    accumulate("a")
    y_step(4, 1)
    deltas.partner_hop(2)
    accumulate("p")
    reduce_last()
    deltas.partner_hop(3)
    deltas.partner_near_done()
    accumulate("pl")
    accumulate("pr")
    deltas.partner_far_done()
    accumulate("pa")
    input_done()

    loads[4].wait()
    loads[5].wait()

    columns(gs)

    def totals(i, squares):
        here = pl.ds(pl.multiple_of(i * 32, 32), 32)
        for k in range(2):
            grad = acc[pl.ds(pl.multiple_of(k * COLS + i * 32, 32), 32), :]
            total = scaled(gc, k, here) + grad
            upd[k, here, :] = total
            squares = squares + jnp.sum((total * total).reshape(4, 8, ROWS), axis=0)
        return squares

    squares = lax.fori_loop(0, COLS // 32, totals, jnp.zeros((8, ROWS), F32))
    part[0] = jnp.broadcast_to(jnp.sum(squares, keepdims=True), (8, 128))
    value = part[0]
    for stage, peer in enumerate((plane_at, z_at, y_at)):
        for k in range(1, 8):
            pltpu.make_async_remote_copy(
                src_ref=part.at[stage],
                dst_ref=parts.at[stage, k - 1],
                send_sem=msend.at[stage],
                recv_sem=mrecv.at[stage],
                device_id=peer(k),
                device_id_type=MESH,
            ).start()
        wait_bytes(parts.at[stage], mrecv.at[stage])
        for k in range(7):
            value = value + parts[stage, k]
        if stage < 2:
            part[stage + 1] = value
    scale[...] = 1.0 / jnp.sqrt(value / (2.0 * D * FF) + 1e-06)

    weights.finish()
    deltas.finish()
    for plane in range(2):
        wait_bytes(xt.at[pl.ds(0, 7 + plane), 0], xsend.at[plane])
    wait_bytes(xt.at[:, pl.ds(0, 7)], ysend)
    wait_bytes(term.at[pl.ds(0, 7)], rsend)
    wait_bytes(zsend, zs_send)
    for stage in range(3):
        wait_bytes(parts.at[stage], msend.at[stage])

def finish(hid, ig, total, scale, hid_o, ig_o, upd_o, upd, sem):
    outs = [pltpu.make_async_copy(hid, hid_o, sem.at[0]), pltpu.make_async_copy(ig, ig_o, sem.at[1])]
    for out in outs:
        out.start()
    factor = scale[0:1, 0:1]
    for half in range(2):

        def normalize(i, carry, half=half):
            here = pl.ds(pl.multiple_of(i * 64, 64), 64)
            upd[half, here, :] = total[half, here, :] * factor
            return carry

        lax.fori_loop(0, COLS // 64, normalize, 0)
        out = pltpu.make_async_copy(upd.at[half], upd_o.at[half], sem.at[2 + half])
        out.start()
        outs.append(out)
    for out in outs:
        out.wait()


def local(tokens, weight_codes, weight_scales, grad_codes, grad_scales, cotangent):
    dma = pltpu.SemaphoreType.DMA
    slots = len(GATHER_SLOTS)
    gather = [dma, dma((slots,)), dma((8,)), dma((8,))]
    call = pl.pallas_call(
        kernel,
        out_shape=(
            pltpu.VMEM((COLS, ROWS), BF16),
            pltpu.VMEM((ROWS, 128), BF16),
            pltpu.VMEM((2, COLS, ROWS), F32),
            pltpu.VMEM((8, 128), F32),
        ),
        in_specs=[pl.BlockSpec(memory_space=pltpu.HBM)] * 6,
        out_specs=[pl.BlockSpec(memory_space=pltpu.VMEM)] * 4,
        scratch_shapes=[
            pltpu.VMEM((ROWS, D), BF16),
            pltpu.VMEM((2, COLS, ROWS), jnp.int32),
            pltpu.VMEM((2, 2, COLS), F32),
            pltpu.VMEM((2, COLS, ROWS), jnp.int32),
            pltpu.VMEM((2, 2, COLS), F32),
            pltpu.VMEM((COLS, ROWS), BF16),
            pltpu.VMEM((16 * CAT, ROWS), BF16),
            pltpu.VMEM((16 * CAT, ROWS), BF16),
            pltpu.VMEM((8, PIECE, ROWS), BF16),
            pltpu.VMEM((8, PIECE, ROWS), BF16),
            pltpu.VMEM((16, 8, 32, ROWS), BF16),
            pltpu.VMEM((CAT, ROWS), F32),
            pltpu.VMEM((8, 4, ROWS, 128), BF16),
            pltpu.VMEM((2, 4, 2, 2, ROWS, 128), BF16),
            pltpu.VMEM((3, ROWS, 128), BF16),
            pltpu.VMEM((3, ROWS, 128), BF16),
            pltpu.VMEM((ROWS, 128), F32),
            pltpu.VMEM((ROWS, CAT), BF16),
            pltpu.VMEM((8, 512), F32),
            pltpu.VMEM((512, 8), F32),
            pltpu.VMEM((3, 8, 128), F32),
            pltpu.VMEM((3, 7, 8, 128), F32),
            dma((6,)),
            *gather,
            *gather,
            dma((2,)),
            dma((2,)),
            dma,
            dma((14,)),
            dma,
            dma((16,)),
            dma,
            dma,
            dma((3,)),
            dma((3,)),
        ],
        compiler_params=pltpu.CompilerParams(
            collective_id=0, has_side_effects=True, vmem_limit_bytes=48 * 1024 * 1024
        ),
    )
    given = (
        tokens,
        weight_codes.transpose(0, 2, 1),
        weight_scales,
        grad_codes.transpose(0, 2, 1),
        grad_scales,
        cotangent.T,
    )
    made = call(*(pltpu.with_memory_space_constraint(a, pltpu.HBM) for a in given))
    hidden, input_grad, update = pl.pallas_call(
        finish,
        out_shape=(
            jax.ShapeDtypeStruct((COLS, ROWS), BF16),
            jax.ShapeDtypeStruct((ROWS, 128), BF16),
            jax.ShapeDtypeStruct((2, COLS, ROWS), F32),
        ),
        in_specs=[pl.BlockSpec(memory_space=pltpu.VMEM)] * 4,
        out_specs=[pl.BlockSpec(memory_space=pltpu.HBM)] * 3,
        scratch_shapes=[pltpu.VMEM((2, COLS, ROWS), F32), dma((4,))],
        compiler_params=pltpu.CompilerParams(vmem_limit_bytes=8 * 1024 * 1024),
    )(*made)
    return hidden.T, input_grad, update.transpose(0, 2, 1)


def solution(mesh):
    finer = Mesh(
        mesh.devices.reshape(4, 8, 2, 4, 2), ("outer_0", "outer_1", "inner_0", "inner_1", "inner_2")
    )
    return jax.shard_map(
        local,
        mesh=finer,
        in_specs=(
            P(INNER, None),
            P(None, INNER, OUTER),
            P(None, INNER, OUTER),
            P(None, INNER, OUTER),
            P(None, INNER, OUTER),
            P(INNER, OUTER),
        ),
        out_specs=(P(INNER, OUTER), P(INNER, OUTER), P(None, INNER, OUTER)),
        check_vma=False,
    )
```

time: 130 us -> 114 us (0.88)
  local copies, waits for them, and re-layouts: 10.6 us -> 0 us
  Pallas kernels: 119 us -> 113 us
    unnamed x8 -> x0, local copies, waits for them, and re-layouts: 6.34 us -> none
    pallas_call x1 -> x2, Pallas kernels: 119 us -> 113 us  [the longest x1 112 us: local(): call(*(pltpu.with_memory_space_constraint(a, pltpu.HBM) for a in given))]
    pallas_call x2 -> x0, local copies, waits for them, and re-layouts: 4.27 us -> none  [local(): call(tokens, weight_codes, weight_scales, grad_codes, grad_scales, cotang...]
where the time goes in v2:
time: 114 us
  Pallas kernels  113 us (99%)
    pallas_call x1, Pallas kernels, local(): call(*(pltpu.with_memory_space_constraint(a, pltpu.HBM) for a in given))  112 us

profile of v2, /device:TPU:1, one launch (start us, length us, event | category | flops | bytes accessed | tf_op | source)
XLA Modules:
  0.0 113.6 jit_solution(17582635995773654435)
XLA Ops:
  0.6 111.7 %shard_map.85 = (bf16[448,256]{1,0:T(8,128)(2,1)S(1)}, bf16[256,128]{1,0:T(8,128)(2,1)S(1)}, f32[2,448,256]{2,1,0:T(8,128)S(1)}, f32[8,128]{1,0:T(8,128)S(1)}) custom-call(bf16[256,4096]{1,0:T(8,128)(2,1)} %tok_h.1, s32[2,448,256]{2,1,0:T(8,128)} %bitcast.5, f32[2,2,448]{2,1,0:T(2,128)} %ws_h.1, s32[2,448,256]{2,1,0:T(8,128)} %bitcast.6, f32[2,2,448]{2,1,0:T(2,128)} %gs_h.1, ...), custom_call_target="tpu_custom_call" | custom-call | tf_op jit(solution)/shard_map/pallas_call | solution.py:709
  112.4 1.2 %shard_map.86 = (bf16[448,256]{1,0:T(8,128)(2,1)}, bf16[256,128]{1,0:T(8,128)(2,1)}, f32[2,448,256]{2,1,0:T(8,128)}) custom-call(bf16[448,256]{1,0:T(8,128)(2,1)S(1)} %get-tuple-element.10.hid, bf16[256,128]{1,0:T(8,128)(2,1)S(1)} %get-tuple-element.11.ig, f32[2,448,256]{2,1,0:T(8,128)S(1)} %get-tuple-element.12.total, f32[8,128]{1,0:T(8,128)S(1)} %get-tuple-element.13.scale), custom_call_target="tpu_custom_call" | custom-call | tf_op jit(solution)/shard_map/pallas_call | solution.py:710

commit v3 on v2

--- a/solution.py
+++ b/solution.py
@@ -18,13 +18,13 @@
 F32 = jnp.float32
 BF16 = jnp.bfloat16
 
-HALF = COLS
+CHUNK = COLS // 2
 PIECE = COLS // 4
 
 GATHER_SLOTS = {
     name: k
     for k, name in enumerate(
-        [f"{b}{h}" for b in ("l", "r", "a") for h in range(2)]
+        [f"{b}{g}{j}" for b in ("l", "r", "a") for g in range(2) for j in range(2)]
         + [f"{b}{q}" for b in ("p", "pl", "pr", "pa") for q in range(8)]
     )
 }
@@ -78,8 +78,8 @@
         where = {"inner_1": self.at["right"] if right else self.at["left"]}
         self.copy(part, part, self.recv.at[GATHER_SLOTS[slot]], where)
 
-    def half(self, role, h):
-        return self.rows(role, h * HALF, HALF)
+    def part(self, role, g, j, sibling=False):
+        return self.rows(role, g * COLS + j * CHUNK, CHUNK, sibling)
 
     def along_z(self, q):
         where = self.at["up2"] if q < 4 else self.at["down2"]
@@ -95,52 +95,56 @@
             dst = self.buf.at[pl.ds(pl.multiple_of(block * CAT + q * PIECE, 16), PIECE)]
             self.copy(self.transit.at[q], dst, self.recv.at[GATHER_SLOTS[f"p{q}"]], where)
 
-    def to_sibling(self, role):
-        part = self.rows(role, 0, CAT)
-        self.copy(part, part, self.sib.at[ROLES.index(role)], {"inner_2": 1 - self.at["c"]})
+    def sibling_sem(self, role, g, j):
+        return self.sib.at[(ROLES.index(role) * 2 + j) * 2 + g]
+
+    def to_sibling(self, role, j):
+        for g in range(2):
+            part = self.part(role, g, j)
+            self.copy(part, part, self.sibling_sem(role, g, j), {"inner_2": 1 - self.at["c"]})
 
     def start_z(self, ks):
         for k in ks:
             self.along_z(k)
             self.along_z(k + 4)
 
-    def start_x(self):
-        self.along_x(self.half("own", 0), True, "l0")
-        self.along_x(self.half("own", 1), False, "r1")
-        self.along_x(self.half("own", 1), True, "l1")
-        self.along_x(self.half("own", 0), False, "r0")
-        self.to_sibling("own")
-
-    def wait_half(self, role, h):
-        wait_bytes(self.half(role, h), self.recv.at[GATHER_SLOTS[f"{role}{h}"]])
+    def start_x(self, j):
+        self.along_x(self.part("own", 0, j), True, f"l0{j}")
+        self.along_x(self.part("own", 1, j), False, f"r1{j}")
+        self.along_x(self.part("own", 1, j), True, f"l1{j}")
+        self.along_x(self.part("own", 0, j), False, f"r0{j}")
+        self.to_sibling("own", j)
+
+    def wait_part(self, role, g, j):
+        wait_bytes(self.part(role, g, j), self.recv.at[GATHER_SLOTS[f"{role}{g}{j}"]])
 
     def wait_piece(self, role, q):
         wait_bytes(self.piece(role, q), self.recv.at[GATHER_SLOTS[f"{role}{q}"]])
 
-    def first_hop(self):
-        self.wait_half("l", 0)
-        self.along_x(self.half("l", 0), True, "a0")
-        self.wait_half("r", 1)
-        self.along_x(self.half("r", 1), False, "a1")
-
-    def near_done(self):
-        self.wait_half("l", 1)
-        self.to_sibling("l")
-        self.wait_half("r", 0)
-        self.to_sibling("r")
-
-    def far_done(self):
-        self.wait_half("a", 0)
-        self.wait_half("a", 1)
-        self.to_sibling("a")
+    def first_hop(self, j):
+        self.wait_part("l", 0, j)
+        self.along_x(self.part("l", 0, j), True, f"a0{j}")
+        self.wait_part("r", 1, j)
+        self.along_x(self.part("r", 1, j), False, f"a1{j}")
+
+    def near_done(self, j):
+        self.wait_part("l", 1, j)
+        self.to_sibling("l", j)
+        self.wait_part("r", 0, j)
+        self.to_sibling("r", j)
+
+    def far_done(self, j):
+        self.wait_part("a", 0, j)
+        self.wait_part("a", 1, j)
+        self.to_sibling("a", j)
 
     def partner(self, k):
         for q in (k, k + 4):
             self.wait_piece("p", q)
             self.along_x(self.piece("p", q), True, f"pl{q}")
             self.along_x(self.piece("p", q), False, f"pr{q}")
-        if k == 3:
-            self.to_sibling("p")
+        if k % 2 == 1:
+            self.to_sibling("p", k // 2)
 
     def partner_hop(self, k):
         self.wait_piece("pl", k)
@@ -148,27 +152,28 @@
         self.wait_piece("pr", k + 4)
         self.along_x(self.piece("pr", k + 4), False, f"pa{k + 4}")
 
-    def partner_near_done(self):
-        for q in range(4, 8):
+    def partner_near_done(self, j):
+        for q in (4 + 2 * j, 5 + 2 * j):
             self.wait_piece("pl", q)
-        self.to_sibling("pl")
-        for q in range(4):
+        self.to_sibling("pl", j)
+        for q in (2 * j, 2 * j + 1):
             self.wait_piece("pr", q)
-        self.to_sibling("pr")
-
-    def partner_far_done(self):
-        for k in range(4):
+        self.to_sibling("pr", j)
+
+    def partner_far_done(self, j):
+        for k in (2 * j, 2 * j + 1):
             self.wait_piece("pa", k)
             self.wait_piece("pa", k + 4)
-        self.to_sibling("pa")
-
-    def blocks(self, role):
+        self.to_sibling("pa", j)
+
+    def blocks(self, role, j):
         c = self.at["c"]
         for k, which in enumerate((c, 1 - c)):
+            parts = [self.part(role, g, j, k == 1) for g in range(2)]
             if k:
-                wait_bytes(self.rows(role, 0, CAT, True), self.sib.at[ROLES.index(role)])
-            number = self.chip[role] * 2 + which
-            yield number, self.block(number)
+                for g in range(2):
+                    wait_bytes(parts[g], self.sibling_sem(role, g, j))
+            yield self.chip[role] * 2 + which, jnp.concatenate([p[...] for p in parts], axis=0)
 
     def block(self, number):
         return self.buf[pl.ds(pl.multiple_of(number * CAT, CAT), CAT), :]
@@ -314,6 +319,7 @@
     dequantize(0)
     pl.semaphore_wait(barrier, len(greeted))
     weights.start_z((0, 1))
+    weights.start_x(0)
     dequantize(COLS // 64)
     weights.start_z((2, 3))
     loads[2].wait()
@@ -339,7 +345,7 @@
             ).start()
 
     exchange_tokens(0)
-    weights.start_x()
+    weights.start_x(1)
     xt[me, y] = tok[own_tokens, pl.ds(pl.multiple_of(me * ROWS, ROWS), ROWS)]
 
     def share_of(k, plane):
@@ -374,69 +380,34 @@
         if s < 3:
             y_share(s, False, 4 + s, plane)
 
-    def multiply(role):
-        for k, (number, block) in enumerate(weights.blocks(role)):
+    def multiply(role, j):
+        for k, (number, block) in enumerate(weights.blocks(role, j)):
             mine = tok[:, pl.ds(pl.multiple_of(number * ROWS, ROWS), ROWS)]
             product = lax.dot_general(
                 block, mine, (((1,), (1,)), ((), ())), preferred_element_type=F32
             )
-            acc[...] = product if role == "own" and k == 0 else acc[...] + product
-
-    multiply("own")
-    weights.pass_on(0)
-    weights.first_hop()
-    weights.pass_on(1)
-    weights.pass_on(2)
-    weights.near_done()
-    exchange_tokens(1)
-    weights.pass_on(3)
-    y_first(0)
-    weights.partner(0)
-    multiply("r")
-    multiply("l")
-    weights.far_done()
-    weights.partner(1)
-    y_step(1, 0)
-    weights.partner_hop(0)
-    weights.partner(2)
-    multiply("a")
-    weights.partner(3)
-    weights.partner_hop(1)
-    y_step(2, 0)
-    y_first(1)
-    weights.partner_hop(2)
-    multiply("p")
-    y_step(3, 0)
-    y_step(1, 1)
-    weights.partner_hop(3)
-    weights.partner_near_done()
-    multiply("pl")
-    multiply("pr")
-    weights.partner_far_done()
-    y_step(4, 0)
-    multiply("pa")
-
-    loads[3].wait()
-
-    def activate(i, carry):
-        here = pl.ds(pl.multiple_of(i * 32, 32), 32)
-        gate = acc[here, :]
-        up = acc[pl.ds(pl.multiple_of(COLS + i * 32, 32), 32), :]
-        back = cot[here, :].astype(F32)
-        sig = jax.nn.sigmoid(gate)
-        d_gate = back * up * sig * (1.0 + gate * (1.0 - sig))
-        d_up = back * gate * sig
-        hid[here, :] = (gate * sig * up).astype(BF16)
-        for k, value in enumerate((d_gate, d_up)):
-            there = pl.ds(pl.multiple_of(own_row + k * COLS + i * 32, 32), 32)
-            dbuf[there, :] = value.astype(BF16)
-        return carry
-
-    lax.fori_loop(0, COLS // 32, activate, 0)
+            acc[j] = product if role == "own" and k == 0 else acc[j] + product
+
+    def activate(j):
+        def some(i, carry):
+            here = pl.ds(pl.multiple_of(j * CHUNK + i * 32, 32), 32)
+            gate = acc[j, pl.ds(pl.multiple_of(i * 32, 32), 32), :]
+            up = acc[j, pl.ds(pl.multiple_of(CHUNK + i * 32, 32), 32), :]
+            back = cot[here, :].astype(F32)
+            sig = jax.nn.sigmoid(gate)
+            d_gate = back * up * sig * (1.0 + gate * (1.0 - sig))
+            d_up = back * gate * sig
+            hid[here, :] = (gate * sig * up).astype(BF16)
+            for k, value in enumerate((d_gate, d_up)):
+                there = pl.ds(
+                    pl.multiple_of(own_row + k * COLS + j * CHUNK + i * 32, 32), 32
+                )
+                dbuf[there, :] = value.astype(BF16)
+            return carry
+
+        lax.fori_loop(0, CHUNK // 32, some, 0)
 
     deltas = Gather(at, dbuf, dtransit, dsend, drecv, drelay, dsib)
-    deltas.start_z(range(4))
-    deltas.start_x()
 
     def partial_inputs(k):
         pair = lax.rem(lax.rem(y + 4, 8) // 2 + k, 4)
@@ -520,12 +491,80 @@
 
         lax.fori_loop(0, ROWS // 64, add, 0)
 
-    def accumulate(role):
-        for k, (number, block) in enumerate(deltas.blocks(role)):
+    def accumulate(role, j):
+        for k, (number, block) in enumerate(deltas.blocks(role, j)):
             product = jnp.dot(
                 block, xt[number].reshape(ROWS, ROWS), preferred_element_type=F32
             )
-            acc[...] = product if role == "own" and k == 0 else acc[...] + product
+            acc[j] = product if role == "own" and k == 0 else acc[j] + product
+
+    def totals(j, squares):
+        def some(i, squares):
+            here = pl.ds(pl.multiple_of(j * CHUNK + i * 32, 32), 32)
+            for k in range(2):
+                grad = acc[j, pl.ds(pl.multiple_of(k * CHUNK + i * 32, 32), 32), :]
+                total = scaled(gc, k, here) + grad
+                upd[k, here, :] = total
+                squares = squares + jnp.sum((total * total).reshape(4, 8, ROWS), axis=0)
+            return squares
+
+        return lax.fori_loop(0, CHUNK // 32, some, squares)
+
+    multiply("own", 0)
+    weights.first_hop(0)
+    multiply("own", 1)
+    weights.pass_on(0)
+    weights.near_done(0)
+    weights.pass_on(1)
+    weights.first_hop(1)
+    weights.pass_on(2)
+    weights.near_done(1)
+    weights.pass_on(3)
+    multiply("r", 0)
+    multiply("l", 0)
+    y_first(0)
+    weights.far_done(0)
+    weights.partner(0)
+    multiply("r", 1)
+    multiply("l", 1)
+    weights.far_done(1)
+    weights.partner(1)
+    y_step(1, 0)
+    multiply("a", 0)
+    weights.partner_hop(0)
+    weights.partner(2)
+    exchange_tokens(1)
+    multiply("a", 1)
+    y_step(2, 0)
+    weights.partner_hop(1)
+    weights.partner(3)
+    multiply("p", 0)
+    weights.partner_near_done(0)
+    multiply("pl", 0)
+    multiply("pr", 0)
+    weights.partner_far_done(0)
+    weights.partner_hop(2)
+    y_step(3, 0)
+    loads[3].wait()
+    multiply("pa", 0)
+    activate(0)
+    deltas.start_z((0, 1))
+    deltas.start_x(0)
+    y_first(1)
+    weights.partner_hop(3)
+    multiply("p", 1)
+    weights.partner_near_done(1)
+    y_step(4, 0)
+    multiply("pl", 1)
+    multiply("pr", 1)
+    deltas.pass_on(0)
+    deltas.first_hop(0)
+    weights.partner_far_done(1)
+    y_step(1, 1)
+    multiply("pa", 1)
+    activate(1)
+    deltas.start_z((2, 3))
+    deltas.start_x(1)
 
     for t in range(CAT // 128):
         there = pl.ds(pl.multiple_of(own_row + t * 128, 128), 128)
@@ -533,67 +572,66 @@
     partial_inputs(0)
     reduce_send(0, 0, 0)
     reduce_send(1, 0, 1)
+    deltas.pass_on(1)
+    deltas.near_done(0)
     partial_inputs(1)
     partial_inputs(3)
     reduce_send(0, 1, 1)
     reduce_send(1, 1, 0)
     y_step(2, 1)
+    deltas.far_done(0)
+    deltas.partner(0)
     partial_inputs(2)
-    deltas.pass_on(0)
+    deltas.first_hop(1)
+    deltas.partner(1)
+    deltas.pass_on(2)
     reduce_step(0, 0, 0)
     reduce_step(1, 0, 1)
-    deltas.first_hop()
-    deltas.pass_on(1)
+    accumulate("own", 0)
+    accumulate("r", 0)
+    accumulate("l", 0)
+    deltas.near_done(1)
+    deltas.pass_on(3)
+    y_step(3, 1)
+    deltas.partner_hop(0)
     reduce_step(0, 1, 1)
     reduce_step(1, 1, 0)
-    deltas.pass_on(2)
-    deltas.near_done()
-    deltas.pass_on(3)
-    y_step(3, 1)
+    accumulate("own", 1)
+    accumulate("a", 0)
+    deltas.far_done(1)
+    deltas.partner(2)
+    deltas.partner_hop(1)
     reduce_step(0, 1, 0)
     reduce_step(1, 1, 1)
-    accumulate("own")
-    deltas.partner(0)
+    accumulate("r", 1)
+    accumulate("l", 1)
+    deltas.partner(3)
+    y_step(4, 1)
+    deltas.partner_near_done(0)
     reduce_step(0, 2, 1)
     reduce_step(1, 2, 0)
-    accumulate("r")
-    deltas.far_done()
-    deltas.partner(1)
-    accumulate("l")
-    deltas.partner_hop(0)
+    accumulate("a", 1)
+    accumulate("p", 0)
+    deltas.partner_hop(2)
+    deltas.partner_far_done(0)
+    accumulate("pl", 0)
+    accumulate("pr", 0)
     reduce_step(0, 2, 0)
     reduce_step(1, 2, 1)
-    deltas.partner(2)
-    deltas.partner_hop(1)
-    deltas.partner(3)
-    accumulate("a")
-    y_step(4, 1)
-    deltas.partner_hop(2)
-    accumulate("p")
-    reduce_last()
+    accumulate("pa", 0)
     deltas.partner_hop(3)
-    deltas.partner_near_done()
-    accumulate("pl")
-    accumulate("pr")
-    deltas.partner_far_done()
-    accumulate("pa")
-    input_done()
-
+    accumulate("p", 1)
     loads[4].wait()
     loads[5].wait()
-
     columns(gs)
-
-    def totals(i, squares):
-        here = pl.ds(pl.multiple_of(i * 32, 32), 32)
-        for k in range(2):
-            grad = acc[pl.ds(pl.multiple_of(k * COLS + i * 32, 32), 32), :]
-            total = scaled(gc, k, here) + grad
-            upd[k, here, :] = total
-            squares = squares + jnp.sum((total * total).reshape(4, 8, ROWS), axis=0)
-        return squares
-
-    squares = lax.fori_loop(0, COLS // 32, totals, jnp.zeros((8, ROWS), F32))
+    deltas.partner_near_done(1)
+    squares = totals(0, jnp.zeros((8, ROWS), F32))
+    accumulate("pl", 1)
+    accumulate("pr", 1)
+    deltas.partner_far_done(1)
+    reduce_last()
+    accumulate("pa", 1)
+    squares = totals(1, squares)
     part[0] = jnp.broadcast_to(jnp.sum(squares, keepdims=True), (8, 128))
     value = part[0]
     for stage, peer in enumerate((plane_at, z_at, y_at)):
@@ -611,6 +649,7 @@
             value = value + parts[stage, k]
         if stage < 2:
             part[stage + 1] = value
+    input_done()
     scale[...] = 1.0 / jnp.sqrt(value / (2.0 * D * FF) + 1e-06)
 
     weights.finish()
@@ -646,7 +685,7 @@
 def local(tokens, weight_codes, weight_scales, grad_codes, grad_scales, cotangent):
     dma = pltpu.SemaphoreType.DMA
     slots = len(GATHER_SLOTS)
-    gather = [dma, dma((slots,)), dma((8,)), dma((8,))]
+    gather = [dma, dma((slots,)), dma((8,)), dma((32,))]
     call = pl.pallas_call(
         kernel,
         out_shape=(
@@ -669,7 +708,7 @@
             pltpu.VMEM((8, PIECE, ROWS), BF16),
             pltpu.VMEM((8, PIECE, ROWS), BF16),
             pltpu.VMEM((16, 8, 32, ROWS), BF16),
-            pltpu.VMEM((CAT, ROWS), F32),
+            pltpu.VMEM((2, COLS, ROWS), F32),
             pltpu.VMEM((8, 4, ROWS, 128), BF16),
             pltpu.VMEM((2, 4, 2, 2, ROWS, 128), BF16),
             pltpu.VMEM((3, ROWS, 128), BF16),

time: 114 us -> 107 us (0.939)
  Pallas kernels: 113 us -> 105 us
    pallas_call x1, Pallas kernels: 112 us -> 104 us  [local(): call(*(pltpu.with_memory_space_constraint(a, pltpu.HBM) for a in given))]
where the time goes in v3:
time: 107 us; the launch traced here: 106 us
  Pallas kernels  105 us (98%)
    pallas_call x1, Pallas kernels, local(): call(*(pltpu.with_memory_space_constraint(a, pltpu.HBM) for a in given))  104 us

profile of v3, /device:TPU:1, one launch (start us, length us, event | category | flops | bytes accessed | tf_op | source)
XLA Modules:
  0.0 106.0 jit_solution(4708615566572835150)
XLA Ops:
  0.6 104.1 %shard_map.85 = (bf16[448,256]{1,0:T(8,128)(2,1)S(1)}, bf16[256,128]{1,0:T(8,128)(2,1)S(1)}, f32[2,448,256]{2,1,0:T(8,128)S(1)}, f32[8,128]{1,0:T(8,128)S(1)}) custom-call(bf16[256,4096]{1,0:T(8,128)(2,1)} %tok_h.1, s32[2,448,256]{2,1,0:T(8,128)} %bitcast.5, f32[2,2,448]{2,1,0:T(2,128)} %ws_h.1, s32[2,448,256]{2,1,0:T(8,128)} %bitcast.6, f32[2,2,448]{2,1,0:T(2,128)} %gs_h.1, ...), custom_call_target="tpu_custom_call" | custom-call | tf_op jit(solution)/shard_map/pallas_call | solution.py:748
  104.7 1.2 %shard_map.86 = (bf16[448,256]{1,0:T(8,128)(2,1)}, bf16[256,128]{1,0:T(8,128)(2,1)}, f32[2,448,256]{2,1,0:T(8,128)}) custom-call(bf16[448,256]{1,0:T(8,128)(2,1)S(1)} %get-tuple-element.10.hid, bf16[256,128]{1,0:T(8,128)(2,1)S(1)} %get-tuple-element.11.ig, f32[2,448,256]{2,1,0:T(8,128)S(1)} %get-tuple-element.12.total, f32[8,128]{1,0:T(8,128)S(1)} %get-tuple-element.13.scale), custom_call_target="tpu_custom_call" | custom-call | tf_op jit(solution)/shard_map/pallas_call | solution.py:749

commit v4 on v3

--- a/solution.py
+++ b/solution.py
@@ -244,14 +244,6 @@
         there = lax.rem(z + k, 8)
         return {"outer_0": lax.rem(there, 4), "inner_0": there // 4}
 
-    def inner_at(k):
-        there = lax.rem(me + k, 16)
-        return there, {
-            "inner_0": there // 8,
-            "inner_1": lax.rem(there // 2, 4),
-            "inner_2": lax.rem(there, 2),
-        }
-
     def plane_at(k):
         there = lax.rem(x * 2 + c + k, 8)
         return {"inner_1": there // 2, "inner_2": lax.rem(there, 2)}
@@ -275,15 +267,18 @@
             ((ws_h, ws), (wc_h, wc), (tok_h, tok), (cot_h, cot), (gs_h, gs), (gc_h, gc))
         )
     ]
-    for load in loads:
+    for load in loads[:2]:
         load.start()
 
     barrier = pltpu.get_barrier_semaphore()
-    greeted = [inner_at(k)[1] for k in range(1, 16)]
-    greeted += [z_at(k) for k in (1, 2, 3, 5, 6, 7)]
-    greeted += [y_at(k) for k in range(1, 8)]
+    greeted = [plane_at(k) for k in range(1, 8)]
+    greeted += [z_at(k) for k in (1, 2, 6, 7)]
+    greeted += [y_at(k) for k in (1, 7)]
     for where in greeted:
         pl.semaphore_signal(barrier, inc=1, device_id=where, device_id_type=MESH)
+
+    for load in loads[2:]:
+        load.start()
 
     loads[0].wait()
     loads[1].wait()
@@ -535,15 +530,15 @@
     weights.partner(2)
     exchange_tokens(1)
     multiply("a", 1)
-    y_step(2, 0)
     weights.partner_hop(1)
     weights.partner(3)
+    y_step(2, 0)
     multiply("p", 0)
     weights.partner_near_done(0)
     multiply("pl", 0)
     multiply("pr", 0)
+    weights.partner_hop(2)
     weights.partner_far_done(0)
-    weights.partner_hop(2)
     y_step(3, 0)
     loads[3].wait()
     multiply("pa", 0)
@@ -559,6 +554,7 @@
     multiply("pr", 1)
     deltas.pass_on(0)
     deltas.first_hop(0)
+    deltas.pass_on(1)
     weights.partner_far_done(1)
     y_step(1, 1)
     multiply("pa", 1)
@@ -572,64 +568,62 @@
     partial_inputs(0)
     reduce_send(0, 0, 0)
     reduce_send(1, 0, 1)
-    deltas.pass_on(1)
     deltas.near_done(0)
     partial_inputs(1)
     partial_inputs(3)
     reduce_send(0, 1, 1)
     reduce_send(1, 1, 0)
-    y_step(2, 1)
     deltas.far_done(0)
     deltas.partner(0)
     partial_inputs(2)
+    y_step(2, 1)
     deltas.first_hop(1)
+    deltas.pass_on(2)
     deltas.partner(1)
-    deltas.pass_on(2)
     reduce_step(0, 0, 0)
     reduce_step(1, 0, 1)
+    deltas.near_done(1)
+    deltas.pass_on(3)
     accumulate("own", 0)
     accumulate("r", 0)
     accumulate("l", 0)
-    deltas.near_done(1)
-    deltas.pass_on(3)
-    y_step(3, 1)
     deltas.partner_hop(0)
     reduce_step(0, 1, 1)
     reduce_step(1, 1, 0)
+    y_step(3, 1)
+    deltas.far_done(1)
+    deltas.partner_hop(1)
+    deltas.partner(2)
+    reduce_step(0, 1, 0)
+    reduce_step(1, 1, 1)
     accumulate("own", 1)
     accumulate("a", 0)
-    deltas.far_done(1)
-    deltas.partner(2)
-    deltas.partner_hop(1)
-    reduce_step(0, 1, 0)
-    reduce_step(1, 1, 1)
+    deltas.partner(3)
+    deltas.partner_near_done(0)
     accumulate("r", 1)
     accumulate("l", 1)
-    deltas.partner(3)
-    y_step(4, 1)
-    deltas.partner_near_done(0)
+    deltas.partner_hop(2)
     reduce_step(0, 2, 1)
     reduce_step(1, 2, 0)
+    deltas.partner_far_done(0)
+    y_step(4, 1)
     accumulate("a", 1)
     accumulate("p", 0)
-    deltas.partner_hop(2)
-    deltas.partner_far_done(0)
+    deltas.partner_hop(3)
     accumulate("pl", 0)
     accumulate("pr", 0)
     reduce_step(0, 2, 0)
     reduce_step(1, 2, 1)
     accumulate("pa", 0)
-    deltas.partner_hop(3)
     accumulate("p", 1)
+    deltas.partner_near_done(1)
     loads[4].wait()
     loads[5].wait()
     columns(gs)
-    deltas.partner_near_done(1)
     squares = totals(0, jnp.zeros((8, ROWS), F32))
     accumulate("pl", 1)
     accumulate("pr", 1)
     deltas.partner_far_done(1)
-    reduce_last()
     accumulate("pa", 1)
     squares = totals(1, squares)
     part[0] = jnp.broadcast_to(jnp.sum(squares, keepdims=True), (8, 128))
@@ -644,6 +638,8 @@
                 device_id=peer(k),
                 device_id_type=MESH,
             ).start()
+        if stage == 0:
+            reduce_last()
         wait_bytes(parts.at[stage], mrecv.at[stage])
         for k in range(7):
             value = value + parts[stage, k]

time: 107 us -> 103 us (0.963)
  Pallas kernels: 105 us -> 102 us
    pallas_call x1, Pallas kernels: 104 us -> 100 us  [local(): call(*(pltpu.with_memory_space_constraint(a, pltpu.HBM) for a in given))]
where the time goes in v4:
time: 103 us; the launch traced here: 102 us
  Pallas kernels  102 us (99%)
    pallas_call x1, Pallas kernels, local(): call(*(pltpu.with_memory_space_constraint(a, pltpu.HBM) for a in given))  100 us

profile of v4, /device:TPU:1, one launch (start us, length us, event | category | flops | bytes accessed | tf_op | source)
XLA Modules:
  0.0 102.2 jit_solution(10569069667806021712)
XLA Ops:
  0.6 100.3 %shard_map.85 = (bf16[448,256]{1,0:T(8,128)(2,1)S(1)}, bf16[256,128]{1,0:T(8,128)(2,1)S(1)}, f32[2,448,256]{2,1,0:T(8,128)S(1)}, f32[8,128]{1,0:T(8,128)S(1)}) custom-call(bf16[256,4096]{1,0:T(8,128)(2,1)} %tok_h.1, s32[2,448,256]{2,1,0:T(8,128)} %bitcast.5, f32[2,2,448]{2,1,0:T(2,128)} %ws_h.1, s32[2,448,256]{2,1,0:T(8,128)} %bitcast.6, f32[2,2,448]{2,1,0:T(2,128)} %gs_h.1, ...), custom_call_target="tpu_custom_call" | custom-call | tf_op jit(solution)/shard_map/pallas_call | solution.py:744
  101.0 1.2 %shard_map.86 = (bf16[448,256]{1,0:T(8,128)(2,1)}, bf16[256,128]{1,0:T(8,128)(2,1)}, f32[2,448,256]{2,1,0:T(8,128)}) custom-call(bf16[448,256]{1,0:T(8,128)(2,1)S(1)} %get-tuple-element.10.hid, bf16[256,128]{1,0:T(8,128)(2,1)S(1)} %get-tuple-element.11.ig, f32[2,448,256]{2,1,0:T(8,128)S(1)} %get-tuple-element.12.total, f32[8,128]{1,0:T(8,128)S(1)} %get-tuple-element.13.scale), custom_call_target="tpu_custom_call" | custom-call | tf_op jit(solution)/shard_map/pallas_call | solution.py:745

commit v5 on v4

--- a/solution.py
+++ b/solution.py
@@ -590,15 +590,15 @@
     deltas.partner_hop(0)
     reduce_step(0, 1, 1)
     reduce_step(1, 1, 0)
-    y_step(3, 1)
+    deltas.partner(2)
     deltas.far_done(1)
     deltas.partner_hop(1)
-    deltas.partner(2)
     reduce_step(0, 1, 0)
     reduce_step(1, 1, 1)
+    deltas.partner(3)
+    y_step(3, 1)
     accumulate("own", 1)
     accumulate("a", 0)
-    deltas.partner(3)
     deltas.partner_near_done(0)
     accumulate("r", 1)
     accumulate("l", 1)
@@ -606,10 +606,10 @@
     reduce_step(0, 2, 1)
     reduce_step(1, 2, 0)
     deltas.partner_far_done(0)
+    accumulate("a", 1)
+    deltas.partner_hop(3)
     y_step(4, 1)
-    accumulate("a", 1)
     accumulate("p", 0)
-    deltas.partner_hop(3)
     accumulate("pl", 0)
     accumulate("pr", 0)
     reduce_step(0, 2, 0)

time: 103 us -> 103 us (level)
  no operation moved by 1% of the time
where the time goes in v5:
time: 103 us
  Pallas kernels  102 us (99%)
    pallas_call x1, Pallas kernels, local(): call(*(pltpu.with_memory_space_constraint(a, pltpu.HBM) for a in given))  101 us

profile of v5, /device:TPU:1, one launch (start us, length us, event | category | flops | bytes accessed | tf_op | source)
XLA Modules:
  0.0 102.7 jit_solution(5772960136195694136)
XLA Ops:
  0.6 100.9 %shard_map.85 = (bf16[448,256]{1,0:T(8,128)(2,1)S(1)}, bf16[256,128]{1,0:T(8,128)(2,1)S(1)}, f32[2,448,256]{2,1,0:T(8,128)S(1)}, f32[8,128]{1,0:T(8,128)S(1)}) custom-call(bf16[256,4096]{1,0:T(8,128)(2,1)} %tok_h.1, s32[2,448,256]{2,1,0:T(8,128)} %bitcast.5, f32[2,2,448]{2,1,0:T(2,128)} %ws_h.1, s32[2,448,256]{2,1,0:T(8,128)} %bitcast.6, f32[2,2,448]{2,1,0:T(2,128)} %gs_h.1, ...), custom_call_target="tpu_custom_call" | custom-call | tf_op jit(solution)/shard_map/pallas_call | solution.py:744
  101.5 1.2 %shard_map.86 = (bf16[448,256]{1,0:T(8,128)(2,1)}, bf16[256,128]{1,0:T(8,128)(2,1)}, f32[2,448,256]{2,1,0:T(8,128)}) custom-call(bf16[448,256]{1,0:T(8,128)(2,1)S(1)} %get-tuple-element.10.hid, bf16[256,128]{1,0:T(8,128)(2,1)S(1)} %get-tuple-element.11.ig, f32[2,448,256]{2,1,0:T(8,128)S(1)} %get-tuple-element.12.total, f32[8,128]{1,0:T(8,128)S(1)} %get-tuple-element.13.scale), custom_call_target="tpu_custom_call" | custom-call | tf_op jit(solution)/shard_map/pallas_call | solution.py:745
